TPU v7x, 256 devices: a whole 4x4x8 slice. The times are simulated.
256 devices in a mesh: blk: 64 (over z, x, core), head: 4 (over y).
Axes of the slice: x: 4, y: 4, z: 8, core: 2. Of those that a mesh axis runs over, the one named last changes fastest.
Arguments:
- layer_input: bfloat16 [32768, 5120], P(('blk', 'head')), may hold values from -0.125 to 0.125
- queries: bfloat16 [32768, 20, 128], P(('blk', 'head')), may hold values from -2 to 2
- key_vectors: bfloat16 [32768, 20, 128], P(('blk', 'head')), may hold values from -2 to 2
- value_vectors: bfloat16 [32768, 20, 128], P(('blk', 'head')), may hold values from -6 to 6
- out_grad: bfloat16 [32768, 20, 128], P(('blk', 'head')), may hold values from -24 to 24
- attn_out: bfloat16 [32768, 20, 128], P(('blk', 'head')), may hold values from -1.796875 to 1.796875
- log_sum: float32 [32768, 20], P(('blk', 'head')), may hold values from 5.5 to 8
- block_list: int32 [256, 8], replicated, may hold values from -1 to 255, as said below
Outputs:
- query_grad: bfloat16 [32768, 20, 128], P(('blk', 'head'))
- key_grad: bfloat16 [32768, 20, 128], P(('blk', 'head'))
- weight_grad: float32 [5120, 2560], P('blk', 'head')
Inputs may be any that keep to these rules, and one draw needn't show every extreme that they name: `block_list`: row r lists distinct key blocks c (blocks of 128 tokens) with |c // 4 - r // 4| <= 1, block r among them, followed by -1 in the unused slots; some row uses all 8 slots.
All inputs are finite; a program needn't handle non-finite values.
Results may differ from a plain program's by a relative error of at most 0.0051.
Values may be sent and summed in bfloat16 or wider, within the bound.
A program may use at most 128 MiB of HBM per device.

v0:
```python
import jax
import jax.numpy as jnp
from jax import lax
from jax.sharding import Mesh
from jax.sharding import PartitionSpec as P

BLOCKS_DEV = 4
BLK = ("blk_0", "blk_1", "blk_2")
BLK_HEAD = ("blk_0", "blk_1", "blk_2", "head")


def side_by_side(arrays, axis, split_dim, concat_dim, along):
    ends, at = ([], 0)
    for a in arrays[:-1]:
        at += a.shape[along]
        ends.append(at)
    both = jnp.concatenate(arrays, axis=along)
    return tuple(
        jnp.split(
            lax.all_to_all(both, axis, split_axis=split_dim, concat_axis=concat_dim, tiled=True),
            ends,
            axis=along,
        )
    )


def with_halo(block, sides, width):
    for axis, dim in sides:
        count = lax.axis_size(axis)
        forward = [(i, i + 1) for i in range(count - 1)]
        backward = [(target, source) for source, target in forward]
        low = lax.ppermute(
            lax.slice_in_dim(block, block.shape[dim] - width, None, axis=dim), axis, forward
        )
        high = lax.ppermute(lax.slice_in_dim(block, 0, width, axis=dim), axis, backward)
        block = jnp.concatenate([low, block, high], axis=dim)
    return block


def shifted(x, axis, by):
    size = lax.axis_size(axis)
    pairs = [(i, i + by) for i in range(size) if 0 <= i + by < size]
    return lax.ppermute(x, axis, pairs)


def sum_by_axis(so_far, axes):
    for axis in axes:
        so_far = lax.psum_scatter(so_far, axis, scatter_dimension=0, tiled=True)
    return so_far


def block_links(listed, block_ids):
    matches = listed[:, :, None] == block_ids[None, None, :]
    return jnp.any(matches, axis=1).astype(jnp.float32)


def tile_grads(queries, out_grad, log_sum, row_delta, key_vectors, value_vectors, block_mask):
    row_count = queries.shape[0]
    column_count = key_vectors.shape[0]
    query_blocks = block_mask.shape[0]
    key_blocks = block_mask.shape[1]
    block_size = row_count // query_blocks
    score_scale = queries.shape[2] ** (-0.5)

    def one_head(member):
        query_head, grad_head, lse_head, delta_head, key_head, value_head = member
        scores = (
            jnp.einsum("qd,kd->qk", query_head, key_head, preferred_element_type=jnp.float32)
            * score_scale
        )
        weights = jnp.exp(scores - lse_head[:, None]).reshape(
            query_blocks, block_size, key_blocks, block_size
        )
        weights = (weights * block_mask[:, None, :, None]).reshape(row_count, column_count)
        dweights = jnp.einsum(
            "qd,kd->qk", grad_head, value_head, preferred_element_type=jnp.float32
        )
        dscores = (weights * (dweights - delta_head[:, None])).astype(jnp.bfloat16)
        weights_b = weights.astype(jnp.bfloat16)
        query_part = (
            jnp.einsum("qk,kd->qd", dscores, key_head, preferred_element_type=jnp.float32)
            * score_scale
        )
        key_part = (
            jnp.einsum("qk,qd->kd", dscores, query_head, preferred_element_type=jnp.float32)
            * score_scale
        )
        value_part = jnp.einsum(
            "qk,qd->kd", weights_b, grad_head, preferred_element_type=jnp.float32
        )
        return (query_part, key_part, value_part)

    by_head = tuple(
        (
            jnp.moveaxis(member, 1, 0)
            for member in (queries, out_grad, log_sum, row_delta, key_vectors, value_vectors)
        )
    )
    results = lax.map(one_head, by_head)
    return tuple((jnp.moveaxis(member, 0, 1) for member in results))


def attend(queries, out_grad, log_sum, row_delta, key_vectors, value_vectors, block_mask):
    return tile_grads(queries, out_grad, log_sum, row_delta, key_vectors, value_vectors, block_mask)


def local(
    layer_input, queries, key_vectors, value_vectors, out_grad, attn_out, log_sum, block_list
):
    row_delta = jnp.sum(out_grad.astype(jnp.float32) * attn_out.astype(jnp.float32), axis=2)
    local_queries, local_keys, local_values, local_grad = side_by_side(
        (queries, key_vectors, value_vectors, out_grad), "head", 1, 0, 2
    )
    local_lse, local_delta = (
        lax.all_to_all(log_sum, "head", split_axis=1, concat_axis=0, tiled=True),
        lax.all_to_all(row_delta, "head", split_axis=1, concat_axis=0, tiled=True),
    )
    gathered = lax.all_gather(layer_input, "head", axis=0, tiled=True)
    length = local_queries.shape[0]
    position = lax.axis_index(BLK)
    first_block = position * BLOCKS_DEV
    padded = jnp.pad(block_list, ((BLOCKS_DEV, BLOCKS_DEV), (0, 0)), constant_values=-1)
    window_lists = lax.dynamic_slice_in_dim(padded, first_block, 3 * BLOCKS_DEV, 0)
    own_ids = first_block + jnp.arange(BLOCKS_DEV, dtype=jnp.int32)
    block_mask = block_links(window_lists, own_ids)
    paired = jnp.stack((local_queries, local_grad))
    window = with_halo(paired, ((BLK, 1),), length)
    statistics = with_halo(jnp.stack((local_lse, local_delta)), ((BLK, 1),), length)
    query_sum, key_total, value_total = attend(
        window[0], window[1], statistics[0], statistics[1], local_keys, local_values, block_mask
    )
    from_right = shifted(query_sum[:length], BLK, -1)
    from_left = shifted(query_sum[2 * length :], BLK, 1)
    query_total = query_sum[length : 2 * length] + from_right + from_left
    query_grad, key_grad = side_by_side(
        (query_total.astype(jnp.bfloat16), key_total.astype(jnp.bfloat16)), "head", 0, 1, 2
    )
    value_rows = value_total.astype(jnp.bfloat16).reshape(length, -1)
    weight_grad = sum_by_axis(
        lax.dot_general(
            gathered, value_rows, (((0,), (0,)), ((), ())), preferred_element_type=jnp.float32
        ),
        BLK,
    )
    return (query_grad, key_grad, weight_grad)


def solution(mesh):
    torus = Mesh(
        mesh.devices.reshape(8, 4, 2, mesh.shape["head"]), ("blk_0", "blk_1", "blk_2", "head")
    )
    placed = (
        P(BLK_HEAD, None),
        P(BLK_HEAD, None, None),
        P(BLK_HEAD, None, None),
        P(BLK_HEAD, None, None),
        P(BLK_HEAD, None, None),
        P(BLK_HEAD, None, None),
        P(BLK_HEAD, None),
        P(),
    )
    return jax.shard_map(
        local,
        mesh=torus,
        in_specs=placed,
        out_specs=(P(BLK_HEAD, None, None), P(BLK_HEAD, None, None), P(BLK, "head")),
        check_vma=False,
    )
```

profile of v0, /device:TPU:3, one launch (start us, length us, event | category | flops | bytes accessed | tf_op | source)
XLA Modules:
  0.0 362.8 jit_solution(5307087458058583970)
XLA Ops:
  7.2 2.0 pad_maximum_fusion.1
  9.2 35.1 %all_to_all.68 = bf16[128,20,512]{2,0,1:T(8,128)(2,1)S(1)} all-to-all(bf16[128,20,512]{2,0,1:T(8,128)(2,1)S(1)} %pad_maximum_fusion.1), channel_id=1, replica_groups=mesh['blk_0'=8,'blk_1'=4,'blk_2'=2,'head'=4] {'head'}, dimensions={1} | all-to-all | bytes 5242880 | tf_op jit(solution)/shard_map/all_to_all | solution.py:20
  45.2 1.2 pad_maximum_fusion.2
  46.4 4.8 %collective-permute-start = (bf16[2,512,5,128]{3,1,2,0:T(8,128)(2,1)}, bf16[2,512,5,128]{3,1,2,0:T(8,128)(2,1)}, u32[]{:S(2)}, u32[]{:S(2)}) collective-permute-start(bf16[2,512,5,128]{3,1,2,0:T(8,128)(2,1)} %pad_maximum_fusion.2), channel_id=1, source_target_pairs={{0,4},{4,8},{8,12},{12,16},{16,20},{20,24},{24,28},{28,32},{32,36}... | collective-permute-start | bytes 3932168 | tf_op jit(solution)/shard_map/ppermute | solution.py:32
  51.2 1.9 collective-permute-start.1
  54.2 3.3 all-to-all-start.2
  58.9 2.7 all-to-all-done.2
  61.7 3.3 all-to-all-start.1
  65.0 4.1 %all-to-all-done.1 = f32[128,4,5]{0,2,1:T(8,128)S(1)} async-done(((f32[128,4,5]{0,2,1:T(8,128)}), f32[128,4,5]{0,2,1:T(8,128)S(1)}, u32[]{:S(2)}, u32[]{:S(2)}) %all-to-all-start.1) | async-done | bytes 10272 | tf_op jit(solution)/shard_map/all_to_all | solution.py:115
  69.1 5.9 %collective-permute-start.2 = (f32[2,512,5]{1,2,0:T(8,128)S(1)}, f32[2,512,5]{1,2,0:T(8,128)S(1)}, u32[]{:S(2)}, u32[]{:S(2)}) collective-permute-start(f32[2,512,5]{1,2,0:T(8,128)S(1)} %pad_maximum_fusion.5), channel_id=1, source_target_pairs={{0,4},{4,8},{8,12},{12,16},{16,20},{20,24},{24,28},{28,32},{32,36}... | collective-permute-start | bytes 61448 | tf_op jit(solution)/shard_map/ppermute | solution.py:32
  75.0 1.9 collective-permute-start.3
  77.2 3.1 collective-permute-done.3
  80.3 3.3 pad_maximum_fusion
  83.6 1.6 slice_bitcast_fusion
  85.2 40.0 %while.14 = (s32[]{:T(128)}, f32[5,1536,128]{2,1,0:T(8,128)}, bf16[5,512,128]{2,1,0:T(8,128)(2,1)}, bf16[5,512,128]{1,2,0:T(8,128)(2,1)}, bf16[5,1536,128]{2,1,0...) while((s32[]{:T(128)}, f32[5,1536,128]{2,1,0:T(8,128)}, ...), condition=%wide.region_3.4_spmd, body=%wide.region_2.3_spmd.sunk | while | flops 1012400128 | bytes 29013360 | solution.py:99
  85.7 1.8 fusion.69
  88.1 1.5 fusion.71
  89.6 1.7 fusion.72
  92.1 1.1 fusion.73
  93.7 1.8 fusion.69
  96.1 1.5 fusion.71
  97.6 1.7 fusion.72
  100.1 1.1 fusion.73
  101.7 1.8 fusion.69
  104.1 1.5 fusion.71
  105.6 1.7 fusion.72
  108.1 1.1 fusion.73
  109.7 1.8 fusion.69
  112.1 1.5 fusion.71
  113.6 1.7 fusion.72
  116.1 1.1 fusion.73
  117.7 1.8 fusion.69
  120.1 1.5 fusion.71
  121.6 1.7 fusion.72
  124.1 1.1 fusion.73
  125.2 11.0 %convolution_bitcast_fusion = f32[5120,640]{0,1:T(8,128)} fusion(bf16[512,640]{0,1:T(8,128)(2,1)} %bitcast.33, bf16[512,5120]{1,0:T(8,128)(2,1)} %all-gather.2.cloned.1.call-done), kind=kOutput, calls=%fused_computation.38 | convolution fusion | flops 3355443200 | bytes 19005440 | tf_op jit(solution)/shard_map/dot_general | solution.py:140
  136.3 145.3 %reduce-scatter.8.cloned.1.call-done = f32[640,640]{0,1:T(8,128)} async-done(((f32[5120,640]{0,1:T(8,128)}), f32[640,640]{0,1:T(8,128)}) %reduce-scatter.8.cloned.1.call-update) | async-done | bytes 1638416 | tf_op jit(solution)/shard_map/reduce_scatter | solution.py:48
  281.6 2.7 copy.40
  284.3 1.9 fusion.38
  286.3 2.8 collective-permute-start.4
  289.1 3.0 collective-permute-start.5
  292.1 22.5 %collective-permute-done.4 = f32[512,5,128]{2,0,1:T(8,128)S(1)} collective-permute-done((f32[512,5,128]{2,0,1:T(8,128)S(1)}, f32[512,5,128]{2,0,1:T(8,128)S(1)}, u32[]{:S(2)}, u32[]{:S(2)}) %collective-permute-start.4) | collective-permute-done | bytes 1310752 | tf_op jit(solution)/shard_map/ppermute | solution.py:43
  314.6 5.2 %collective-permute-done.5 = f32[512,5,128]{2,0,1:T(8,128)S(1)} collective-permute-done((f32[512,5,128]{2,0,1:T(8,128)S(1)}, f32[512,5,128]{2,0,1:T(8,128)S(1)}, u32[]{:S(2)}, u32[]{:S(2)}) %collective-permute-start.5) | collective-permute-done | bytes 1310752 | tf_op jit(solution)/shard_map/ppermute | solution.py:43
  319.8 1.6 fusion.37
  321.5 2.2 copy.36
  323.7 4.0 %all-to-all-start.3 = ((bf16[512,5,256]{2,1,0:T(8,128)(2,1)}), bf16[512,5,256]{2,1,0:T(8,128)(2,1)S(1)}, u32[]{:S(2)}, u32[]{:S(2)}) async-start(bf16[512,5,256]{2,1,0:T(8,128)(2,1)} %copy.36), calls=%async_computation.3 | async-start | bytes 4194304 | tf_op jit(solution)/shard_map/all_to_all | solution.py:20
  328.2 26.2 %all-to-all-done.3 = bf16[512,5,256]{2,1,0:T(8,128)(2,1)S(1)} async-done(((bf16[512,5,256]{2,1,0:T(8,128)(2,1)}), bf16[512,5,256]{2,1,0:T(8,128)(2,1)S(1)}, u32[]{:S(2)}, u32[]{:S(2)}) %all-to-all-start.3) | async-done | bytes 1310752 | tf_op jit(solution)/shard_map/all_to_all | solution.py:20
  354.8 1.4 fusion.39
  (77 shorter events, 14.4 us)
Async XLA Ops:
  45.2 8.0 %copy-start = (bf16[128,20,128]{2,0,1:T(8,128)(2,1)S(1)}, bf16[128,20,128]{2,0,1:T(8,128)(2,1)}, u32[]{:S(2)}) copy-start(bf16[128,20,128]{2,0,1:T(8,128)(2,1)} %param.14) | copy-start | bytes 1966084
  45.2 8.0 %copy-start.4 = (bf16[128,20,128]{2,0,1:T(8,128)(2,1)S(1)}, bf16[128,20,128]{2,0,1:T(8,128)(2,1)}, u32[]{:S(2)}) copy-start(bf16[128,20,128]{2,0,1:T(8,128)(2,1)} %param.15) | copy-start | bytes 1966084
  45.2 13.0 %copy-start.6 = (s32[256,8]{0,1:T(8,128)S(1)}, s32[256,8]{0,1:T(8,128)}, u32[]{:S(2)}) copy-start(s32[256,8]{0,1:T(8,128)} %param.17) | copy-start | bytes 24580
  45.2 13.1 %copy-start.5 = (f32[128,20]{0,1:T(8,128)S(1)}, f32[128,20]{0,1:T(8,128)}, u32[]{:S(2)}) copy-start(f32[128,20]{0,1:T(8,128)} %param.16) | copy-start | bytes 30724
  46.4 33.9 %collective-permute-start = (bf16[2,512,5,128]{3,1,2,0:T(8,128)(2,1)}, bf16[2,512,5,128]{3,1,2,0:T(8,128)(2,1)}, u32[]{:S(2)}, u32[]{:S(2)}) collective-permute-start(bf16[2,512,5,128]{3,1,2,0:T(8,128)(2,1)} %pad_maximum_fusion.2), channel_id=1, source_target_pairs={{0,4},{4,8},{8,12},{12,16},{16,20},{20,24},{24,28},{28,32},{32,36}... | collective-permute-start | bytes 3932168 | tf_op jit(solution)/shard_map/ppermute | solution.py:32
  51.2 29.1 %collective-permute-start.1 = (bf16[2,512,5,128]{3,1,2,0:T(8,128)(2,1)}, bf16[2,512,5,128]{3,1,2,0:T(8,128)(2,1)}, u32[]{:S(2)}, u32[]{:S(2)}) collective-permute-start(bf16[2,512,5,128]{3,1,2,0:T(8,128)(2,1)} %pad_maximum_fusion.2), channel_id=1, source_target_pairs={{4,0},{8,4},{12,8},{16,12},{20,16},{24,20},{28,24},{32,28},{36,32}... | collective-permute-start | bytes 3932168 | tf_op jit(solution)/shard_map/ppermute | solution.py:35
  54.2 7.4 %all-to-all-start.2 = ((f32[128,4,5]{0,2,1:T(8,128)}), f32[128,4,5]{0,2,1:T(8,128)S(1)}, u32[]{:S(2)}, u32[]{:S(2)}) async-start(f32[128,4,5]{0,2,1:T(8,128)} %all_to_all.57), calls=%async_computation.2 | async-start | bytes 32768 | tf_op jit(solution)/shard_map/all_to_all | solution.py:116
  57.5 67.7 %all-gather.2.cloned.1.call-start = ((), (), s32[]{:S(2)}) async-start(), calls=%async_computation.7 | async-start | bytes 6553600 | tf_op jit(solution)/shard_map/all_gather | solution.py:118
  61.7 7.4 %all-to-all-start.1 = ((f32[128,4,5]{0,2,1:T(8,128)}), f32[128,4,5]{0,2,1:T(8,128)S(1)}, u32[]{:S(2)}, u32[]{:S(2)}) async-start(f32[128,4,5]{0,2,1:T(8,128)} %all_to_all.54), calls=%async_computation.1 | async-start | bytes 32768 | tf_op jit(solution)/shard_map/all_to_all | solution.py:115
  64.9 216.7 %reduce-scatter.8.cloned.1.call-start = ((), (), s32[]{:S(2)}) async-start(), calls=%async_computation.8 | async-start | bytes 14745600 | tf_op jit(solution)/shard_map/reduce_scatter | solution.py:48
  69.1 8.1 %collective-permute-start.2 = (f32[2,512,5]{1,2,0:T(8,128)S(1)}, f32[2,512,5]{1,2,0:T(8,128)S(1)}, u32[]{:S(2)}, u32[]{:S(2)}) collective-permute-start(f32[2,512,5]{1,2,0:T(8,128)S(1)} %pad_maximum_fusion.5), channel_id=1, source_target_pairs={{0,4},{4,8},{8,12},{12,16},{16,20},{20,24},{24,28},{28,32},{32,36}... | collective-permute-start | bytes 61448 | tf_op jit(solution)/shard_map/ppermute | solution.py:32
  75.0 5.2 %collective-permute-start.3 = (f32[2,512,5]{1,2,0:T(8,128)S(1)}, f32[2,512,5]{1,2,0:T(8,128)S(1)}, u32[]{:S(2)}, u32[]{:S(2)}) collective-permute-start(f32[2,512,5]{1,2,0:T(8,128)S(1)} %pad_maximum_fusion.5), channel_id=1, source_target_pairs={{4,0},{8,4},{12,8},{16,12},{20,16},{24,20},{28,24},{32,28},{36,32}... | collective-permute-start | bytes 61448 | tf_op jit(solution)/shard_map/ppermute | solution.py:35
  87.5 2.1 copy-start.1
  91.3 0.8 copy-start.2
  95.5 2.1 copy-start.1
  99.3 0.8 copy-start.2
  103.5 2.1 copy-start.1
  107.3 0.8 copy-start.2
  111.5 2.1 copy-start.1
  115.3 0.8 copy-start.2
  119.5 2.1 copy-start.1
  123.3 0.8 copy-start.2
  136.2 191.5 %reduce-scatter.10.cloned.1.call-start = ((), (), s32[]{:S(2)}) async-start(), calls=%async_computation.9 | async-start | bytes 2048000
  286.3 35.1 %copy-start.3 = (bf16[5,512,128]{2,1,0:T(8,128)(2,1)S(1)}, bf16[5,512,128]{2,1,0:T(8,128)(2,1)}, u32[]{:S(2)}) copy-start(bf16[5,512,128]{2,1,0:T(8,128)(2,1)} %get-tuple-element.63) | copy-start | bytes 1966084
  286.3 28.3 %collective-permute-start.4 = (f32[512,5,128]{2,0,1:T(8,128)S(1)}, f32[512,5,128]{2,0,1:T(8,128)S(1)}, u32[]{:S(2)}, u32[]{:S(2)}) collective-permute-start(f32[512,5,128]{2,0,1:T(8,128)S(1)} %get-tuple-element.115), channel_id=1, source_target_pairs={{4,0},{8,4},{12,8},{16,12},{20,16},{24,20},{28,24},{32,28},{36,32}... | collective-permute-start | bytes 3932168 | tf_op jit(solution)/shard_map/ppermute | solution.py:43
  289.1 30.7 %collective-permute-start.5 = (f32[512,5,128]{2,0,1:T(8,128)S(1)}, f32[512,5,128]{2,0,1:T(8,128)S(1)}, u32[]{:S(2)}, u32[]{:S(2)}) collective-permute-start(f32[512,5,128]{2,0,1:T(8,128)S(1)} %get-tuple-element.116), channel_id=1, source_target_pairs={{0,4},{4,8},{8,12},{12,16},{16,20},{20,24},{24,28},{28,32},{32,36}... | collective-permute-start | bytes 3932168 | tf_op jit(solution)/shard_map/ppermute | solution.py:43
  323.7 30.8 %all-to-all-start.3 = ((bf16[512,5,256]{2,1,0:T(8,128)(2,1)}), bf16[512,5,256]{2,1,0:T(8,128)(2,1)S(1)}, u32[]{:S(2)}, u32[]{:S(2)}) async-start(bf16[512,5,256]{2,1,0:T(8,128)(2,1)} %copy.36), calls=%async_computation.3 | async-start | bytes 4194304 | tf_op jit(solution)/shard_map/all_to_all | solution.py:20
  327.7 28.5 %reduce-scatter.12.cloned.1.call-start = ((), (), s32[]{:S(2)}) async-start(), calls=%async_computation.10 | async-start | bytes 614400
Sparse Core Ops, SparseCore 0:
  60.1 63.3 all-gather.1
  136.3 145.2 reduce-scatter.7
  284.5 36.6 reduce-scatter.9
  331.2 13.6 reduce-scatter.11
where the time goes:
time: 364 us; the launch traced here: 363 us
  waiting for transfers between devices  210 us (58%)
  matrix products  44 us (12%)
  blocking collectives  35.1 us (10%)
  starting transfers between devices  31 us (9%)
  local copies, waits for them, and re-layouts  19.2 us (5%)
  between operations  14 us (4%)
  other arithmetic  8.79 us (2%)
    reduce_scatter x1, waiting for transfers between devices, sum_by_axis(): so_far = lax.psum_scatter(so_far, axis, scatter_dimension=0, tiled=True)  145 us
    all_to_all x1, blocking collectives, side_by_side(): lax.all_to_all(both, axis, split_axis=split_dim, concat_axis=concat_dim,...  35.1 us
    ppermute x2, waiting for transfers between devices, shifted(): return lax.ppermute(x, axis, pairs)  27.7 us
    all_to_all x1, waiting for transfers between devices, side_by_side(): lax.all_to_all(both, axis, split_axis=split_dim, concat_axis=concat_dim,...  26.2 us
    dot_general x1, matrix products, local(): lax.dot_general(gathered, value_rows, (((0,), (0,)), ((), ())), preferred...  11 us
    ppermute x2, starting transfers between devices, with_halo(): lax.ppermute(lax.slice_in_dim(block, block.shape[dim] - width, None, axis...  10.7 us
    dot_general x5, matrix products, one_head(): jnp.einsum('qd,kd->qk', query_head, key_head, preferred_element_type=jnp....  8.88 us
    dot_general x5, matrix products, one_head(): jnp.einsum('qk,qd->kd', dscores, query_head, preferred_element_type=jnp.f...  8.35 us
  transfers between devices with their start and end apart: 13, of which 7 were waited for; matrix products, arithmetic and copies ran while one was open for 13% of the time, Pallas kernels for 0%

commit v1 on v0

v1 whole, which is shorter than its diff:
```python
import jax
import jax.numpy as jnp
from jax import lax
from jax.experimental import pallas as pl
from jax.experimental.pallas import tpu as pltpu
from jax.sharding import PartitionSpec as P

F32 = jnp.float32
BF16 = jnp.bfloat16
MESH = pl.DeviceIdType.MESH
SPAN = 512
TILE = 128
HEADS = 5
CHUNK = 256
HALF = 320
COLS = 640
N_BLK = 64
SCALE = 128 ** -0.5
FAR = 1e30
ORDER = (2, 1, 3, 0)


def push(src, dst, send, recv, **where):
    return pltpu.make_async_remote_copy(
        src_ref=src,
        dst_ref=dst,
        send_sem=send,
        recv_sem=recv,
        device_id=where,
        device_id_type=MESH,
    )


def meet(peers):
    barrier = pltpu.get_barrier_semaphore()
    for where in peers:
        pl.semaphore_signal(barrier, inc=1, device_id=where, device_id_type=MESH)
    pl.semaphore_wait(barrier, len(peers))


def rows(start):
    return pl.ds(pl.multiple_of(start, TILE), TILE)


def around(y):
    return lax.rem(y + 1, 4), lax.rem(y + 3, 4), lax.rem(y + 2, 4)


def entry_kernel(
    qg, kv_in, stat_in, lt, win, kv, stat, lt_x, relay,
    y_send, y_recv, s_send, s_recv, h_send, h_recv, t_send, t_recv, l_send, l_recv,
):
    b = lax.axis_index("blk")
    y = lax.axis_index("head")
    yr, yl, y2 = around(y)
    br, bl = lax.rem(b + 1, N_BLK), lax.rem(b + N_BLK - 1, N_BLK)
    core = lax.rem(b, 2)
    mate = b + 1 - 2 * core
    meet(
        [{"blk": b, "head": yr}, {"blk": b, "head": yl}, {"blk": b, "head": y2}]
        + [{"blk": br, "head": y}, {"blk": bl, "head": y}]
    )

    def mine(ref, to):
        return ref.at[:, pl.ds(to * HEADS, HEADS)]

    def one(ref, t, to):
        return ref.at[t, pl.ds(to * HEADS, HEADS)]

    def first(phase, src, dst, base):
        sends = []
        for i, (where, copy_from, copy_to) in enumerate(
            (
                (yr, one(src, 0, y2), relay.at[phase, 0]),
                (yl, one(src, 1, y2), relay.at[phase, 1]),
                (yr, mine(src, yr), dst.at[:, :, rows(base + y * TILE)]),
                (yl, mine(src, yl), dst.at[:, :, rows(base + y * TILE)]),
            )
        ):
            sends.append(
                push(copy_from, copy_to, y_send.at[phase, i], y_recv.at[phase, i], blk=b, head=where)
            )
            sends[-1].start()
        return sends

    def second(phase, sends, dst, base):
        sends[0].wait_recv()
        sends.append(
            push(
                relay.at[phase, 0], dst.at[0, :, rows(base + yl * TILE)],
                y_send.at[phase, 4], y_recv.at[phase, 4], blk=b, head=yr,
            )
        )
        sends[-1].start()
        sends[1].wait_recv()
        sends.append(
            push(
                relay.at[phase, 1], dst.at[1, :, rows(base + yr * TILE)],
                y_send.at[phase, 5], y_recv.at[phase, 5], blk=b, head=yl,
            )
        )
        sends[-1].start()

    stat_sends = []
    for i, where in enumerate((yr, yl, y2)):
        stat_sends.append(
            push(stat_in.at[where], stat.at[4 + y], s_send.at[i], s_recv.at[i], blk=b, head=where)
        )
        stat_sends[-1].start()
    queries = first(0, qg, win, SPAN)
    halo = []

    def pass_on(i, src, stat_src, owner):
        for j, (where, base, at) in enumerate(((br, 0, 0), (bl, 2 * SPAN, 8))):
            halo.append(
                push(
                    src, win.at[:, :, rows(base + owner * TILE)],
                    h_send.at[i, j], h_recv.at[i, j], blk=where, head=y,
                )
            )
            halo[-1].start()
            halo.append(
                push(
                    stat_src, stat.at[at + owner],
                    t_send.at[i, j], t_recv.at[i, j], blk=where, head=y,
                )
            )
            halo[-1].start()

    pass_on(0, mine(qg, y), stat_in.at[y], y)
    lt_copy = push(lt.at[:, 1 - core], lt_x, l_send, l_recv, blk=mate, head=y)
    lt_copy.start()
    for t in range(2):
        for h in range(HEADS):
            win[t, h, rows(SPAN + y * TILE)] = qg[t, y * HEADS + h]
            kv[t, h, rows(y * TILE)] = kv_in[t, y * HEADS + h]
    stat[4 + y] = stat_in[y]
    second(0, queries, win, SPAN)
    keys = first(1, kv_in, kv, 0)
    for i, owner in ((2, yl), (3, yr)):
        queries[i].wait_recv()
        stat_sends[i - 2].wait_recv()
        pass_on(i - 1, win.at[:, :, rows(SPAN + owner * TILE)], stat.at[4 + owner], owner)
    queries[4].wait_recv()
    queries[5].wait_recv()
    stat_sends[2].wait_recv()
    pass_on(3, win.at[:, :, rows(SPAN + y2 * TILE)], stat.at[4 + y2], y2)
    second(1, keys, kv, 0)
    for copy in keys[2:] + halo:
        copy.wait_recv()
    lt_copy.wait_recv()
    for copy in queries + keys + stat_sends + halo + [lt_copy]:
        copy.wait_send()


def dot(a, b, contract):
    return lax.dot_general(a, b, (contract, ((), ())), preferred_element_type=F32)


def main_kernel(
    win, kv, stat, far, lt, lt_x, grads, weight,
    gathered, dq, dk, dv, values, dq_out, dq_in, back, relay,
    x2_out, x2_in, xr_out, xr_in, xl_out, xl_in, total, z_out, z_in,
    own_sem, g_send, g_recv, v_send, v_recv, q_send, q_recv,
    x_send, x_recv, z_send, z_recv, b_send, b_recv,
):
    b = lax.axis_index("blk")
    y = lax.axis_index("head")
    yr, yl, y2 = around(y)
    br, bl = lax.rem(b + 1, N_BLK), lax.rem(b + N_BLK - 1, N_BLK)
    core = lax.rem(b, 2)
    mate = b + 1 - 2 * core
    x = lax.rem(b // 2, 4)
    z = b // 8
    xr = z * 8 + lax.rem(x + 1, 4) * 2 + core
    xl = z * 8 + lax.rem(x + 3, 4) * 2 + core

    def pair(owner):
        return pl.ds(pl.multiple_of(owner * 256, 256), 256)

    def lane(c):
        return pl.ds(pl.multiple_of(y * 256 + c * 128, 128), 128)

    own = []
    for i, dx in enumerate(ORDER):
        to = lax.rem(x + dx, 4)
        own.append(
            (
                pltpu.make_async_copy(lt.at[to, core], gathered.at[i, :, :, lane(core)], own_sem.at[i, 0]),
                pltpu.make_async_copy(lt_x.at[to], gathered.at[i, :, :, lane(1 - core)], own_sem.at[i, 1]),
            )
        )
        own[-1][0].start()
        own[-1][1].start()
    meet(
        [{"blk": b, "head": yr}, {"blk": b, "head": yl}, {"blk": b, "head": y2}]
        + [{"blk": br, "head": y}, {"blk": bl, "head": y}]
        + [{"blk": xr, "head": y}, {"blk": xl, "head": y}]
        + [{"blk": lax.rem(b + 8 * r, N_BLK), "head": y} for r in range(1, 8)]
    )
    gathers = {}

    def spread(i):
        own[i][0].wait()
        own[i][1].wait()
        for j, where in enumerate((yr, yl)):
            piece = gathered.at[i, :, :, pair(y)]
            gathers[i, j] = push(
                piece, piece, g_send.at[i, j], g_recv.at[i, j], blk=b, head=where
            )
            gathers[i, j].start()

    def forward(i):
        for j, (where, owner) in enumerate(((yr, yl), (yl, yr))):
            gathers[i, j].wait_recv()
            piece = gathered.at[i, j, :, pair(owner)]
            gathers[i, 2 + j] = push(
                piece, piece, g_send.at[i, 2 + j], g_recv.at[i, 2 + j], blk=b, head=where
            )
            gathers[i, 2 + j].start()

    def complete(i):
        gathers[i, 2].wait_recv()
        gathers[i, 3].wait_recv()

    def attend(step, carry):
        h = step // 6
        part = lax.rem(step, 6)
        at = pl.ds(pl.multiple_of(part * CHUNK, CHUNK), CHUNK)
        keys, vals = kv[0, h], kv[1, h]
        queries, grad = win[0, h, at], win[1, h, at]
        lo, hi = stat[2 * part, h], stat[2 * part + 1, h]
        far_lo, far_hi = far[2 * part], far[2 * part + 1]
        lse = jnp.concatenate([lo[0:1], hi[0:1]], axis=1)
        delta = jnp.concatenate([lo[1:2], hi[1:2]], axis=1)
        apart = jnp.concatenate([far_lo[0:4], far_hi[0:4]], axis=1) + lse
        scores = dot(keys, queries, ((1,), (1,))) * SCALE
        dweights = dot(vals, grad, ((1,), (1,)))
        weights = jnp.concatenate(
            [
                jnp.exp(scores[k * TILE : (k + 1) * TILE] - apart[k : k + 1])
                for k in range(4)
            ],
            axis=0,
        )
        dscores = (weights * (dweights - delta)).astype(BF16)
        weights = weights.astype(BF16)
        value_part = dot(weights, grad, ((1,), (0,)))
        key_part = dot(dscores, queries, ((1,), (0,)))
        dq[h, at] = dot(dscores, keys, ((0,), (0,))) * SCALE

        @pl.when(part == 0)
        def _():
            dv[h] = value_part
            dk[h] = key_part

        @pl.when(part != 0)
        def _():
            dv[h] += value_part
            dk[h] += key_part

        return carry

    spread(0)
    spread(1)
    lax.fori_loop(0, 18, attend, 0)
    forward(0)
    spread(2)
    lax.fori_loop(18, 30, attend, 0)
    forward(1)
    spread(3)

    for h in range(HEADS):
        cols = pl.ds(h * 128, 128)
        for k in range(4):
            values[k, core, :, cols] = dv[h, k * TILE : (k + 1) * TILE].astype(BF16)
    value_copy = push(
        values.at[:, core], values.at[:, core], v_send, v_recv, blk=mate, head=y
    )
    value_copy.start()
    for h in range(HEADS):
        dq_out[0, h] = dq[h, 0:SPAN].astype(BF16)
        dq_out[1, h] = dq[h, 2 * SPAN :].astype(BF16)
    dq_copies = []
    for j, where in enumerate((bl, br)):
        dq_copies.append(
            push(dq_out.at[j], dq_in.at[j], q_send.at[j], q_recv.at[j], blk=where, head=y)
        )
        dq_copies[-1].start()
    for h in range(HEADS):
        back[1, h] = (dk[h] * SCALE).astype(BF16)
    value_copy.wait_recv()

    def product(i, half):
        return dot(
            gathered[i, half], values[...].reshape(1024, COLS), ((1,), (0,))
        )

    complete(0)
    x_copies = []

    def x_push(i, src, dst, where):
        x_copies.append(push(src, dst, x_send.at[i], x_recv.at[i], blk=where, head=y))
        x_copies[-1].start()

    x2_out[0] = product(0, 0).astype(BF16)
    x_push(0, x2_out.at[0], x2_in.at[0], xr)
    x2_out[1] = product(0, 1).astype(BF16)
    x_push(1, x2_out.at[1], x2_in.at[1], xl)
    for copy in dq_copies:
        copy.wait_recv()
    for h in range(HEADS):
        back[0, h] = (
            dq[h, SPAN : 2 * SPAN] + dq_in[0, h].astype(F32) + dq_in[1, h].astype(F32)
        ).astype(BF16)
    forward(2)
    complete(1)
    first_half = product(1, 0)
    x_copies[0].wait_recv()
    xr_out[0] = (first_half + x2_in[0].astype(F32)).astype(BF16)
    x_push(2, xr_out.at[0], xr_in.at[0], xr)
    xr_out[1] = product(1, 1).astype(BF16)
    x_push(3, xr_out.at[1], xr_in.at[1], xr)
    forward(3)
    complete(2)
    xl_out[0] = product(2, 0).astype(BF16)
    x_push(4, xl_out.at[0], xl_in.at[0], xl)
    second_half = product(2, 1)
    x_copies[1].wait_recv()
    xl_out[1] = (second_half + x2_in[1].astype(F32)).astype(BF16)
    x_push(5, xl_out.at[1], xl_in.at[1], xl)

    back_copies = []
    for i, (where, copy_from, copy_to) in enumerate(
        (
            (yr, back.at[0, :, rows(y2 * TILE)], relay.at[0]),
            (yl, back.at[1, :, rows(y2 * TILE)], relay.at[1]),
            (yr, back.at[:, :, rows(yr * TILE)], grads.at[:, pl.ds(y * HEADS, HEADS)]),
            (yl, back.at[:, :, rows(yl * TILE)], grads.at[:, pl.ds(y * HEADS, HEADS)]),
        )
    ):
        back_copies.append(
            push(copy_from, copy_to, b_send.at[i], b_recv.at[i], blk=b, head=where)
        )
        back_copies[-1].start()
    for t in range(2):
        for h in range(HEADS):
            grads[t, y * HEADS + h] = back[t, h, rows(y * TILE)]
    complete(3)
    total[0] = product(3, 0)
    total[1] = product(3, 1)
    for j, (where, owner) in enumerate(((yr, yl), (yl, yr))):
        back_copies[j].wait_recv()
        back_copies.append(
            push(
                relay.at[j], grads.at[j, pl.ds(owner * HEADS, HEADS)],
                b_send.at[4 + j], b_recv.at[4 + j], blk=b, head=where,
            )
        )
        back_copies[-1].start()

    def sum_half(half):
        summed = total[half] + xr_in[half].astype(F32) + xl_in[half].astype(F32)
        total[half] = summed
        z_out[half] = summed.astype(BF16)

    def z_push(half):
        for k in range(4):
            to = 2 * k + half

            @pl.when(z != to)
            def _():
                push(
                    z_out.at[half, pl.ds(k * 80, 80)], z_in.at[lax.rem(to - z + 8, 8)],
                    z_send.at[lax.rem(to - z + 8, 8)], z_recv.at[lax.rem(to - z + 8, 8)],
                    blk=to * 8 + x * 2 + core, head=y,
                ).start()

    x_copies[2].wait_recv()
    x_copies[4].wait_recv()
    sum_half(0)
    z_push(0)
    x_copies[3].wait_recv()
    x_copies[5].wait_recv()
    sum_half(1)
    z_push(1)
    result = total[lax.rem(z, 2), pl.ds(pl.multiple_of((z // 2) * 80, 80), 80)]
    for r in range(1, 8):
        copy = push(
            z_out.at[0, pl.ds(0, 80)], z_in.at[r], z_send.at[r], z_recv.at[r],
            blk=lax.rem(b + 8 * r, N_BLK), head=y,
        )
        copy.wait_recv()
        result = result + z_in[r].astype(F32)
        copy.wait_send()
    weight[...] = result
    for copy in back_copies[2:]:
        copy.wait_recv()
    for copy in back_copies + x_copies + dq_copies + [value_copy] + list(gathers.values()):
        copy.wait_send()


VMEM_SPEC = pl.BlockSpec(memory_space=pltpu.VMEM)
ANY_SPEC = pl.BlockSpec(memory_space=pl.ANY)


def sems(*shape):
    return pltpu.SemaphoreType.DMA(shape) if shape else pltpu.SemaphoreType.DMA


def local(
    layer_input, queries, key_vectors, value_vectors, out_grad, attn_out, log_sum, block_list
):
    row_delta = jnp.sum(out_grad.astype(F32) * attn_out.astype(F32), axis=2)
    stats = jnp.stack((log_sum.T, row_delta.T), axis=1)
    stats = jnp.pad(stats, ((0, 0), (0, 6), (0, 0))).reshape(4, HEADS, 8, TILE)
    qg = jnp.stack((jnp.swapaxes(queries, 0, 1), jnp.swapaxes(out_grad, 0, 1)))
    kv = jnp.stack((jnp.swapaxes(key_vectors, 0, 1), jnp.swapaxes(value_vectors, 0, 1)))
    lt = layer_input.T.reshape(4, 2, 4, 2, 80, TILE)
    lt = jnp.transpose(lt, (2, 3, 1, 0, 4, 5)).reshape(4, 2, 2, HALF, TILE)

    first_block = lax.axis_index("blk") * 4
    padded = jnp.pad(block_list, ((4, 4), (0, 0)), constant_values=-1)
    lists = lax.dynamic_slice_in_dim(padded, first_block, 12, 0)
    own_ids = first_block + jnp.arange(8, dtype=jnp.int32)
    allowed = jnp.any(lists[:, None, :] == own_ids[None, :, None], axis=2)
    far = jnp.broadcast_to(jnp.where(allowed, 0.0, FAR)[:, :, None], (12, 8, TILE)).astype(F32)

    win, kv_all, stat, lt_x = pl.pallas_call(
        entry_kernel,
        out_shape=(
            jax.ShapeDtypeStruct((2, HEADS, 3 * SPAN, 128), BF16),
            jax.ShapeDtypeStruct((2, HEADS, SPAN, 128), BF16),
            jax.ShapeDtypeStruct((12, HEADS, 8, TILE), F32),
            jax.ShapeDtypeStruct((4, 2, HALF, TILE), BF16),
        ),
        in_specs=[VMEM_SPEC] * 3 + [ANY_SPEC],
        out_specs=[VMEM_SPEC] * 3 + [ANY_SPEC],
        scratch_shapes=[
            pltpu.VMEM((2, 2, HEADS, TILE, 128), BF16),
            sems(2, 6), sems(2, 6), sems(3), sems(3), sems(4, 2), sems(4, 2),
            sems(4, 2), sems(4, 2), sems(), sems(),
        ],
        compiler_params=pltpu.CompilerParams(
            collective_id=0, has_side_effects=True, vmem_limit_bytes=60 * 2**20
        ),
        name="entry",
    )(qg, kv, stats, lt)

    grads, weight = pl.pallas_call(
        main_kernel,
        out_shape=(
            jax.ShapeDtypeStruct((2, 20, TILE, 128), BF16),
            jax.ShapeDtypeStruct((80, COLS), F32),
        ),
        in_specs=[VMEM_SPEC] * 4 + [ANY_SPEC] * 2,
        out_specs=[VMEM_SPEC] * 2,
        scratch_shapes=[
            pltpu.VMEM((4, 2, HALF, 1024), BF16),
            pltpu.VMEM((HEADS, 3 * SPAN, 128), F32),
            pltpu.VMEM((HEADS, SPAN, 128), F32),
            pltpu.VMEM((HEADS, SPAN, 128), F32),
            pltpu.VMEM((4, 2, TILE, COLS), BF16),
            pltpu.VMEM((2, HEADS, SPAN, 128), BF16),
            pltpu.VMEM((2, HEADS, SPAN, 128), BF16),
            pltpu.VMEM((2, HEADS, SPAN, 128), BF16),
            pltpu.VMEM((2, HEADS, TILE, 128), BF16),
        ]
        + [pltpu.VMEM((2, HALF, COLS), BF16)] * 6
        + [
            pltpu.VMEM((2, HALF, COLS), F32),
            pltpu.VMEM((2, HALF, COLS), BF16),
            pltpu.VMEM((8, 80, COLS), BF16),
            sems(4, 2), sems(4, 4), sems(4, 4), sems(), sems(), sems(2), sems(2),
            sems(6), sems(6), sems(8), sems(8), sems(6), sems(6),
        ],
        compiler_params=pltpu.CompilerParams(
            collective_id=1, has_side_effects=True, vmem_limit_bytes=60 * 2**20
        ),
        name="main",
    )(win, kv_all, stat, far, lt, lt_x)
    return (jnp.swapaxes(grads[0], 0, 1), jnp.swapaxes(grads[1], 0, 1), weight)


def solution(mesh):
    both = ("blk", "head")
    rows3 = P(both, None, None)
    return jax.shard_map(
        local,
        mesh=mesh,
        in_specs=(P(both, None),) + (rows3,) * 5 + (P(both, None), P()),
        out_specs=(rows3, rows3, P("blk", "head")),
        check_vma=False,
    )
```

time: 364 us -> 134 us (0.37)
  waiting for transfers between devices: 210 us -> 0 us
  Pallas kernels: 0 us -> 121 us
  matrix products: 44 us -> 0 us
  blocking collectives: 35.1 us -> 0 us
  starting transfers between devices: 31 us -> 0 us
  between operations: 14 us -> 0.73 us
  local copies, waits for them, and re-layouts: 19.2 us -> 7 us
  other arithmetic: 8.79 us -> 4.1 us
    reduce_scatter x1 -> x0, waiting for transfers between devices: 145 us -> none  [sum_by_axis(): so_far = lax.psum_scatter(so_far, axis, scatter_dimension=0, tiled=True)]
    pallas_call x0 -> x2, Pallas kernels: none -> 121 us  [the longest x1 81.6 us: local(): pl.pallas_call(main_kernel, out_shape=(jax.ShapeDtypeStruct((2, 20, TILE,...]
    dot_general x26 -> x0, matrix products: 44 us -> none  [the longest x1 11 us: local(): lax.dot_general(gathered, value_rows, (((0,), (0,)), ((), ())), preferred...]
    all_to_all x1 -> x0, blocking collectives: 35.1 us -> none  [side_by_side(): lax.all_to_all(both, axis, split_axis=split_dim, concat_axis=concat_dim,...]
    all_to_all x3 -> x0, waiting for transfers between devices: 33.1 us -> none  [the longest x1 26.2 us: side_by_side(): lax.all_to_all(both, axis, split_axis=split_dim, concat_axis=concat_dim,...]
    ppermute x6 -> x0, waiting for transfers between devices: 30.8 us -> none  [the longest x2 27.7 us: shifted(): return lax.ppermute(x, axis, pairs)]
    ppermute x6 -> x0, starting transfers between devices: 20.4 us -> none  [the longest x2 10.7 us: with_halo(): lax.ppermute(lax.slice_in_dim(block, block.shape[dim] - width, None, axis...]
    all_to_all x3 -> x0, starting transfers between devices: 10.5 us -> none  [the longest x1 3.99 us: side_by_side(): lax.all_to_all(both, axis, split_axis=split_dim, concat_axis=concat_dim,...]
  transfers between devices with their start and end apart: 13 -> 0, of which waited for: 7 -> 0; matrix products, arithmetic and copies ran while one was open for 13% -> 0% of each run, Pallas kernels for 0% -> 0%
where the time goes in v1:
time: 134 us; the launch traced here: 133 us
  Pallas kernels  121 us (90%)
  local copies, waits for them, and re-layouts  7 us (5%)
  other arithmetic  4.1 us (3%)
    pallas_call x1, Pallas kernels, local(): pl.pallas_call(main_kernel, out_shape=(jax.ShapeDtypeStruct((2, 20, TILE,...  81.6 us
    pallas_call x1, Pallas kernels, local(): pl.pallas_call(entry_kernel, out_shape=(jax.ShapeDtypeStruct((2, HEADS, 3...  39.1 us
    another operation x1, other arithmetic, local(): qg = jnp.stack((jnp.swapaxes(queries, 0, 1), jnp.swapaxes(out_grad, 0, 1)))  3.57 us

profile of v1, /device:TPU:3, one launch (start us, length us, event | category | flops | bytes accessed | tf_op | source)
XLA Modules:
  0.0 132.5 jit_solution(14183799642779571878)
XLA Ops:
  0.6 0.0 copy-start
  0.6 0.0 copy-start.2
  0.7 3.6 %pad_maximum_fusion = (bf16[2,20,128,128]{3,2,1,0:T(8,128)(2,1)}, bf16[2,20,128,128]{3,2,1,0:T(8,128)(2,1)}) fusion(bf16[1,20,128,128]{3,2,1,0:T(8,128)(2,1)} %bitcast.36, bf16[1,20,128,128]{3,2,1,0:T(8,128)(2,1)} %bitcast.37, bf16[1,20,128,128]{3,2,1,0:T(8,128)(2,1)} %bitcast.38, bf16[1,20,128,128]{3,2,1,0:T(8,128)(2,1)} %bitcast.39), kind=kLoop, calls=%fused_computation | loop fusion | flops 1310720 | bytes 5242880 | tf_op jit(solution)/shard_map/stack | solution.py:417
  4.2 0.0 copy-start.4
  4.2 0.0 copy-start.1
  4.2 0.0 copy-done
  4.2 0.0 copy-done.2
  4.2 0.4 multiply_reduce_fusion
  4.7 0.3 copy-done.4
  5.0 0.6 pad.8.clone
  5.6 0.0 copy-done.1
  5.6 0.8 copy.19
  6.4 1.2 copy.20
  7.6 0.0 copy-start.5
  7.6 39.1 %entry.1 = (bf16[2,5,1536,128]{3,2,1,0:T(8,128)(2,1)}, bf16[2,5,512,128]{3,2,1,0:T(8,128)(2,1)}, f32[12,5,8,128]{3,2,1,0:T(8,128)}, bf16[4,2,320,128]{3,2,1,0:T(8,128)(2,1)}) custom-call(bf16[2,20,128,128]{3,2,1,0:T(8,128)(2,1)} %get-tuple-element.17.qg, bf16[2,20,128,128]{3,2,1,0:T(8,128)(2,1)} %get-tuple-element.18.kv_in, f32[4,5,8,128]{3,2,1,0:T(8,128)} %bitcast.40, ...), custom_call_target="tpu_custom_call" | custom-call | tf_op jit(solution)/shard_map/entry/pallas_call | solution.py:429
  46.7 0.0 copy-done.5
  46.7 0.1 pad_dynamic-slice_fusion
  46.8 0.1 compare_reduce_fusion
  46.9 0.1 copy.21
  47.0 0.7 broadcast_in_dim.18.far
  47.7 81.6 %main.1 = (bf16[2,20,128,128]{3,2,1,0:T(8,128)(2,1)}, f32[80,640]{1,0:T(8,128)}) custom-call(bf16[2,5,1536,128]{3,2,1,0:T(8,128)(2,1)} %get-tuple-element.9.win, bf16[2,5,512,128]{3,2,1,0:T(8,128)(2,1)} %get-tuple-element.10.kv, f32[12,5,8,128]{3,2,1,0:T(8,128)} %get-tuple-element.11.stat, f32[12,8,128]{2,1,0:T(8,128)} %broadcast_in_dim.18.far, ...), custom_call_target="tpu_custom_call" | custom-call | tf_op jit(solution)/shard_map/main/pallas_call | solution.py:450
  129.3 0.0 copy-start.3
  129.3 2.5 %slice_bitcast_fusion = (bf16[128,20,128]{2,0,1:T(8,128)(2,1)}, bf16[128,20,128]{2,0,1:T(8,128)(2,1)}) fusion(bf16[2,20,128,128]{3,2,1,0:T(8,128)(2,1)} %get-tuple-element.13), kind=kLoop, calls=%fused_computation.3 | loop fusion | bytes 2621440 | tf_op jit(solution)/shard_map/transpose | solution.py:482
  131.9 0.0 copy-done.3
  131.9 0.7 copy.24
  (4 shorter events, 0.0 us)
Async XLA Ops:
  0.6 3.6 %copy-start = (bf16[128,20,128]{2,0,1:T(8,128)(2,1)S(1)}, bf16[128,20,128]{2,0,1:T(8,128)(2,1)}, u32[]{:S(2)}) copy-start(bf16[128,20,128]{2,0,1:T(8,128)(2,1)} %param.12) | copy-start | bytes 1966084
  0.6 3.6 %copy-start.2 = (bf16[128,20,128]{2,0,1:T(8,128)(2,1)S(1)}, bf16[128,20,128]{2,0,1:T(8,128)(2,1)}, u32[]{:S(2)}) copy-start(bf16[128,20,128]{2,0,1:T(8,128)(2,1)} %param.13) | copy-start | bytes 1966084
  4.2 0.7 copy-start.4
  4.2 1.4 %copy-start.1 = (bf16[128,5120]{1,0:T(8,128)(2,1)S(1)}, bf16[128,5120]{1,0:T(8,128)(2,1)}, u32[]{:S(2)}) copy-start(bf16[128,5120]{1,0:T(8,128)(2,1)} %param.8) | copy-start | bytes 3932164
  7.6 39.1 %copy-start.5 = (s32[256,8]{0,1:T(8,128)S(1)}, s32[256,8]{0,1:T(8,128)}, u32[]{:S(2)}) copy-start(s32[256,8]{0,1:T(8,128)} %param.15) | copy-start | bytes 24580
  129.3 2.5 %copy-start.3 = (f32[80,640]{1,0:T(8,128)S(1)}, f32[80,640]{1,0:T(8,128)}, u32[]{:S(2)}) copy-start(f32[80,640]{1,0:T(8,128)} %get-tuple-element.24) | copy-start | bytes 614404

commit v2 on v0

v2 whole, which is shorter than its diff:
```python
import jax
import jax.numpy as jnp
from jax import lax
from jax.experimental import pallas as pl
from jax.experimental.pallas import tpu as pltpu
from jax.sharding import PartitionSpec as P

F32 = jnp.float32
BF16 = jnp.bfloat16
MESH = pl.DeviceIdType.MESH
SPAN = 512
TILE = 128
HEADS = 5
HALF = 320
COLS = 640
N_BLK = 64
SCALE = 128 ** -0.5
FAR = 1e30
ORDER = (2, 1, 3, 0)


def push(src, dst, send, recv, **where):
    return pltpu.make_async_remote_copy(
        src_ref=src,
        dst_ref=dst,
        send_sem=send,
        recv_sem=recv,
        device_id=where,
        device_id_type=MESH,
    )


def meet(peers):
    barrier = pltpu.get_barrier_semaphore()
    for where in peers:
        pl.semaphore_signal(barrier, inc=1, device_id=where, device_id_type=MESH)
    pl.semaphore_wait(barrier, len(peers))


def rows(start):
    return pl.ds(pl.multiple_of(start, TILE), TILE)


def around(y):
    return lax.rem(y + 1, 4), lax.rem(y + 3, 4), lax.rem(y + 2, 4)


def dot(a, b, contract):
    return lax.dot_general(a, b, (contract, ((), ())), preferred_element_type=F32)


def kernel(
    q_in, g_in, k_in, v_in, stat_in, far, lt, grads, weight,
    win, kv, stat, entry_relay, gathered, dq, dk, dv, values, dq_out, dq_in, back, relay,
    x2_out, x2_in, xr_out, xr_in, xl_out, xl_in, total, z_out, z_in,
    y_send, y_recv, s_send, s_recv, h_send, h_recv, t_send, t_recv, l_send, l_recv,
    own_sem, g_send, g_recv, v_send, v_recv, q_send, q_recv,
    x_send, x_recv, z_send, z_recv, b_send, b_recv,
):
    b = lax.axis_index("blk")
    y = lax.axis_index("head")
    yr, yl, y2 = around(y)
    br, bl = lax.rem(b + 1, N_BLK), lax.rem(b + N_BLK - 1, N_BLK)
    core = lax.rem(b, 2)
    mate = b + 1 - 2 * core
    x = lax.rem(b // 2, 4)
    z = b // 8
    xr = z * 8 + lax.rem(x + 1, 4) * 2 + core
    xl = z * 8 + lax.rem(x + 3, 4) * 2 + core

    def pair(owner):
        return pl.ds(pl.multiple_of(owner * 256, 256), 256)

    lane = pl.ds(pl.multiple_of(y * 256 + core * 128, 128), 128)
    turn = pl.ds(lax.rem(z + 3, 8), 8)
    own = []
    for i, dx in enumerate(ORDER):
        source = lt.at[lax.rem(x + dx, 4), core, turn]
        own.append(pltpu.make_async_copy(source, gathered.at[i, :, :, lane], own_sem.at[i]))
        own[-1].start()
    meet(
        [{"blk": b, "head": yr}, {"blk": b, "head": yl}, {"blk": b, "head": y2}]
        + [{"blk": br, "head": y}, {"blk": bl, "head": y}]
        + [{"blk": xr, "head": y}, {"blk": xl, "head": y}]
        + [{"blk": lax.rem(b + 8 * r, N_BLK), "head": y} for r in range(1, 8)]
    )

    def mine(ref, to):
        return ref.at[pl.ds(to * HEADS, HEADS)]

    def first(phase, srcs, dst, base):
        at = rows(base + y * TILE)
        plan = [
            (yr, mine(srcs[0], y2), entry_relay.at[phase, 0]),
            (yl, mine(srcs[1], y2), entry_relay.at[phase, 1]),
        ]
        for t in range(2):
            for where in (yr, yl):
                plan.append((where, mine(srcs[t], where), dst.at[t, :, at]))
        sends = []
        for i, (where, copy_from, copy_to) in enumerate(plan):
            sends.append(
                push(copy_from, copy_to, y_send.at[phase, i], y_recv.at[phase, i], blk=b, head=where)
            )
            sends[-1].start()
        return sends

    def second(phase, sends, dst, base):
        for j, (where, owner) in enumerate(((yr, yl), (yl, yr))):
            sends[j].wait_recv()
            sends.append(
                push(
                    entry_relay.at[phase, j], dst.at[j, :, rows(base + owner * TILE)],
                    y_send.at[phase, 6 + j], y_recv.at[phase, 6 + j], blk=b, head=where,
                )
            )
            sends[-1].start()

    stat_sends = []
    for i, where in enumerate((yr, yl, y2)):
        stat_sends.append(
            push(stat_in.at[where], stat.at[4 + y], s_send.at[i], s_recv.at[i], blk=b, head=where)
        )
        stat_sends[-1].start()
    keys = first(0, (k_in, v_in), kv, 0)
    halo = []

    def pass_on(i, srcs, stat_src, owner):
        for j, (where, base, at) in enumerate(((br, 0, 0), (bl, 2 * SPAN, 8))):
            for t in range(2):
                halo.append(
                    push(
                        srcs[t], win.at[t, :, rows(base + owner * TILE)],
                        h_send.at[i, j, t], h_recv.at[i, j, t], blk=where, head=y,
                    )
                )
                halo[-1].start()
            halo.append(
                push(
                    stat_src, stat.at[at + owner],
                    t_send.at[i, j], t_recv.at[i, j], blk=where, head=y,
                )
            )
            halo[-1].start()

    def landed(owner):
        return [win.at[t, :, rows(SPAN + owner * TILE)] for t in range(2)]

    pass_on(0, [mine(q_in, y), mine(g_in, y)], stat_in.at[y], y)
    swaps = []
    for i, dx in enumerate(ORDER):
        swaps.append(
            push(
                lt.at[lax.rem(x + dx, 4), 1 - core, turn], gathered.at[i, :, :, lane],
                l_send.at[i], l_recv.at[i], blk=mate, head=y,
            )
        )
        swaps[-1].start()
    for h in range(HEADS):
        for t, (near, key) in enumerate(((q_in, k_in), (g_in, v_in))):
            win[t, h, rows(SPAN + y * TILE)] = near[y * HEADS + h]
            kv[t, h, rows(y * TILE)] = key[y * HEADS + h]
    stat[4 + y] = stat_in[y]
    second(0, keys, kv, 0)
    queries = first(1, (q_in, g_in), win, SPAN)

    pieces = ((0, 0), (0, 1), (1, 0), (2, 0), (3, 0), (1, 1), (2, 1), (3, 1))
    gathers = {}
    for i in range(4):
        own[i].wait()

    def spread(p):
        i, half = pieces[p]
        if p in (0, 2, 3, 4):
            swaps[i].wait_recv()
        for j, where in enumerate((yr, yl)):
            piece = gathered.at[i, pl.ds(4 * half, 4), :, pair(y)]
            gathers[p, j] = push(
                piece, piece, g_send.at[p, j], g_recv.at[p, j], blk=b, head=where
            )
            gathers[p, j].start()

    def forward(p):
        i, half = pieces[p]
        for j, (where, owner) in enumerate(((yr, yl), (yl, yr))):
            gathers[p, j].wait_recv()
            piece = gathered.at[i, pl.ds(4 * half + 2 * j, 2), :, pair(owner)]
            gathers[p, 2 + j] = push(
                piece, piece, g_send.at[p, 2 + j], g_recv.at[p, 2 + j], blk=b, head=where
            )
            gathers[p, 2 + j].start()

    def product(p):
        i, half = pieces[p]
        gathers[p, 2].wait_recv()
        gathers[p, 3].wait_recv()
        left = gathered[i, 4 * half : 4 * half + 4].reshape(HALF, 1024)
        return dot(left, values[...].reshape(1024, COLS), ((1,), (0,)))

    def attend(owner, lead):
        spans = [rows(part * SPAN + owner * TILE) for part in range(3)]

        def one_head(h, carry):
            key, val = kv[0, h], kv[1, h]
            query = jnp.concatenate([win[0, h, at] for at in spans], axis=0)
            grad = jnp.concatenate([win[1, h, at] for at in spans], axis=0)
            tiles = [stat[4 * part + owner, h] for part in range(3)]
            lse = jnp.concatenate([tile[0:1] for tile in tiles], axis=1)
            delta = jnp.concatenate([tile[1:2] for tile in tiles], axis=1)
            apart = jnp.concatenate([far[4 * part + owner, 0:4] for part in range(3)], axis=1) + lse
            scores = dot(key, query, ((1,), (1,))) * SCALE
            dweights = dot(val, grad, ((1,), (1,)))
            weights = jnp.concatenate(
                [
                    jnp.exp(scores[k * TILE : (k + 1) * TILE] - apart[k : k + 1])
                    for k in range(4)
                ],
                axis=0,
            )
            dscores = (weights * (dweights - delta)).astype(BF16)
            weights = weights.astype(BF16)
            value_part = dot(weights, grad, ((1,), (0,)))
            key_part = dot(dscores, query, ((1,), (0,)))
            query_part = dot(dscores, key, ((0,), (0,))) * SCALE
            dq_out[0, h, rows(owner * TILE)] = query_part[:TILE].astype(BF16)
            dq[h, rows(owner * TILE)] = query_part[TILE : 2 * TILE]
            dq_out[1, h, rows(owner * TILE)] = query_part[2 * TILE :].astype(BF16)
            if lead:
                dv[h] = value_part
                dk[h] = key_part
            else:
                dv[h] += value_part
                dk[h] += key_part
            return carry

        lax.fori_loop(0, HEADS, one_head, 0)

    dq_copies = []

    def send_dq(i, owner):
        for j, where in enumerate((bl, br)):
            piece = (j, slice(None), rows(owner * TILE))
            dq_copies.append(
                push(
                    dq_out.at[piece], dq_in.at[piece],
                    q_send.at[i, j], q_recv.at[i, j], blk=where, head=y,
                )
            )
            dq_copies[-1].start()

    def halo_in(i):
        for copy in halo[6 * i : 6 * i + 6]:
            copy.wait_recv()

    for copy in keys[2:]:
        copy.wait_recv()
    second(1, queries, win, SPAN)
    spread(0)
    spread(1)
    spread(2)
    halo_in(0)
    attend(y, True)
    for i, owner in ((0, yl), (1, yr)):
        queries[2 + i].wait_recv()
        queries[4 + i].wait_recv()
        stat_sends[i].wait_recv()
        pass_on(1 + i, landed(owner), stat.at[4 + owner], owner)
    send_dq(0, y)
    halo_in(1)
    attend(yl, False)
    queries[6].wait_recv()
    queries[7].wait_recv()
    stat_sends[2].wait_recv()
    pass_on(3, landed(y2), stat.at[4 + y2], y2)
    send_dq(1, yl)
    halo_in(2)
    attend(yr, False)
    send_dq(2, yr)
    forward(0)
    spread(3)
    halo_in(3)
    attend(y2, False)

    for h in range(HEADS):
        cols = pl.ds(h * 128, 128)
        for k in range(4):
            values[k, core, :, cols] = dv[h, k * TILE : (k + 1) * TILE].astype(BF16)
    value_copy = push(
        values.at[:, core], values.at[:, core], v_send, v_recv, blk=mate, head=y
    )
    value_copy.start()
    send_dq(3, y2)
    forward(1)
    forward(2)
    spread(4)
    forward(3)
    spread(5)
    value_copy.wait_recv()
    x_copies = {}

    def x_push(name, i, q, src, dst, where):
        copy = push(src.at[q], dst.at[q], x_send.at[i, q], x_recv.at[i, q], blk=where, head=y)
        copy.start()
        x_copies[name, q] = copy

    def quarters(value):
        return ((0, value[:160]), (1, value[160:]))

    for q, part in quarters(product(0)):
        x2_out[q] = part.astype(BF16)
        x_push("far", 0, q, x2_out, x2_in, xr)
    for q, part in quarters(product(1)):
        x2_out[2 + q] = part.astype(BF16)
        x_push("far", 0, 2 + q, x2_out, x2_in, xl)
    for h in range(HEADS):
        back[1, h] = (dk[h] * SCALE).astype(BF16)
    forward(4)
    spread(6)
    for q, part in quarters(product(2)):
        x_copies["far", q].wait_recv()
        xr_out[q] = (part + x2_in[q].astype(F32)).astype(BF16)
        x_push("right", 1, q, xr_out, xr_in, xr)
    for q, part in quarters(product(3)):
        xl_out[q] = part.astype(BF16)
        x_push("left", 2, q, xl_out, xl_in, xl)
    forward(5)
    spread(7)
    total[0:HALF] = product(4)
    for q, part in quarters(product(5)):
        xr_out[2 + q] = part.astype(BF16)
        x_push("right", 1, 2 + q, xr_out, xr_in, xr)
    forward(6)
    for q, part in quarters(product(6)):
        x_copies["far", 2 + q].wait_recv()
        xl_out[2 + q] = (part + x2_in[2 + q].astype(F32)).astype(BF16)
        x_push("left", 2, 2 + q, xl_out, xl_in, xl)
    forward(7)

    for copy in dq_copies:
        copy.wait_recv()
    for h in range(HEADS):
        back[0, h] = (
            dq[h] + dq_in[0, h].astype(F32) + dq_in[1, h].astype(F32)
        ).astype(BF16)
    back_copies = []
    for i, (where, copy_from, copy_to) in enumerate(
        (
            (yr, back.at[0, :, rows(y2 * TILE)], relay.at[0]),
            (yl, back.at[1, :, rows(y2 * TILE)], relay.at[1]),
            (yr, back.at[:, :, rows(yr * TILE)], grads.at[:, pl.ds(y * HEADS, HEADS)]),
            (yl, back.at[:, :, rows(yl * TILE)], grads.at[:, pl.ds(y * HEADS, HEADS)]),
        )
    ):
        back_copies.append(
            push(copy_from, copy_to, b_send.at[i], b_recv.at[i], blk=b, head=where)
        )
        back_copies[-1].start()
    for t in range(2):
        for h in range(HEADS):
            grads[t, y * HEADS + h] = back[t, h, rows(y * TILE)]

    z_copies = {}

    def reduce_quarter(q):
        x_copies["right", q].wait_recv()
        x_copies["left", q].wait_recv()
        at = pl.ds(160 * q, 160)
        summed = total[at] + xr_in[q].astype(F32) + xl_in[q].astype(F32)
        for k in range(2):
            r = (3 + 2 * q + k) % 8
            part = summed[80 * k : 80 * k + 80]
            if r == 0:
                weight[...] = part
                continue
            z_out[r] = part.astype(BF16)
            z_copies[r] = push(
                z_out.at[r], z_in.at[r], z_send.at[r], z_recv.at[r],
                blk=lax.rem(b + 8 * r, N_BLK), head=y,
            )
            z_copies[r].start()

    reduce_quarter(0)
    reduce_quarter(1)
    total[HALF : 2 * HALF] = product(7)
    reduce_quarter(2)
    for j, (where, owner) in enumerate(((yr, yl), (yl, yr))):
        back_copies[j].wait_recv()
        back_copies.append(
            push(
                relay.at[j], grads.at[j, pl.ds(owner * HEADS, HEADS)],
                b_send.at[4 + j], b_recv.at[4 + j], blk=b, head=where,
            )
        )
        back_copies[-1].start()

    reduce_quarter(3)
    result = weight[...]
    for r in (3, 4, 5, 6, 7, 1, 2):
        z_copies[r].wait_recv()
        result = result + z_in[r].astype(F32)
    weight[...] = result
    for copy in back_copies[2:]:
        copy.wait_recv()
    copies = queries + keys + stat_sends + halo + swaps + list(gathers.values())
    copies += list(x_copies.values()) + list(z_copies.values())
    for copy in copies + [value_copy] + dq_copies + back_copies:
        copy.wait_send()


VMEM_SPEC = pl.BlockSpec(memory_space=pltpu.VMEM)
ANY_SPEC = pl.BlockSpec(memory_space=pl.ANY)


def sems(*shape):
    return pltpu.SemaphoreType.DMA(shape) if shape else pltpu.SemaphoreType.DMA


def local(
    layer_input, queries, key_vectors, value_vectors, out_grad, attn_out, log_sum, block_list
):
    row_delta = jnp.sum(out_grad.astype(F32) * attn_out.astype(F32), axis=2)
    stats = jnp.stack((log_sum.T, row_delta.T), axis=1)
    stats = jnp.pad(stats, ((0, 0), (0, 6), (0, 0))).reshape(4, HEADS, 8, TILE)
    by_head = [
        jnp.swapaxes(array, 0, 1) for array in (queries, out_grad, key_vectors, value_vectors)
    ]
    lt = jnp.transpose(layer_input.T.reshape(8, 4, 2, 80, TILE), (1, 2, 0, 3, 4))
    lt = jnp.concatenate((lt, lt), axis=2)

    first_block = lax.axis_index("blk") * 4
    padded = jnp.pad(block_list, ((4, 4), (0, 0)), constant_values=-1)
    lists = lax.dynamic_slice_in_dim(padded, first_block, 12, 0)
    own_ids = first_block + jnp.arange(8, dtype=jnp.int32)
    allowed = jnp.any(lists[:, None, :] == own_ids[None, :, None], axis=2)
    far = jnp.broadcast_to(jnp.where(allowed, 0.0, FAR)[:, :, None], (12, 8, TILE)).astype(F32)

    grads, weight = pl.pallas_call(
        kernel,
        out_shape=(
            jax.ShapeDtypeStruct((2, 20, TILE, 128), BF16),
            jax.ShapeDtypeStruct((80, COLS), F32),
        ),
        in_specs=[VMEM_SPEC] * 6 + [ANY_SPEC],
        out_specs=[VMEM_SPEC] * 2,
        scratch_shapes=[
            pltpu.VMEM((2, HEADS, 3 * SPAN, 128), BF16),
            pltpu.VMEM((2, HEADS, SPAN, 128), BF16),
            pltpu.VMEM((12, HEADS, 8, TILE), F32),
            pltpu.VMEM((2, 2, HEADS, TILE, 128), BF16),
            pltpu.VMEM((4, 8, 80, 1024), BF16),
            pltpu.VMEM((HEADS, SPAN, 128), F32),
            pltpu.VMEM((HEADS, SPAN, 128), F32),
            pltpu.VMEM((HEADS, SPAN, 128), F32),
            pltpu.VMEM((4, 2, TILE, COLS), BF16),
            pltpu.VMEM((2, HEADS, SPAN, 128), BF16),
            pltpu.VMEM((2, HEADS, SPAN, 128), BF16),
            pltpu.VMEM((2, HEADS, SPAN, 128), BF16),
            pltpu.VMEM((2, HEADS, TILE, 128), BF16),
        ]
        + [pltpu.VMEM((4, 160, COLS), BF16)] * 6
        + [
            pltpu.VMEM((2 * HALF, COLS), F32),
            pltpu.VMEM((8, 80, COLS), BF16),
            pltpu.VMEM((8, 80, COLS), BF16),
            sems(2, 8), sems(2, 8), sems(3), sems(3), sems(4, 2, 2), sems(4, 2, 2),
            sems(4, 2), sems(4, 2), sems(4), sems(4),
            sems(4), sems(8, 4), sems(8, 4), sems(), sems(), sems(4, 2), sems(4, 2),
            sems(3, 4), sems(3, 4), sems(8), sems(8), sems(6), sems(6),
        ],
        compiler_params=pltpu.CompilerParams(
            collective_id=0, has_side_effects=True, vmem_limit_bytes=60 * 2**20
        ),
        name="layer",
    )(*by_head, stats, far, lt)
    return (jnp.swapaxes(grads[0], 0, 1), jnp.swapaxes(grads[1], 0, 1), weight)


def solution(mesh):
    both = ("blk", "head")
    rows3 = P(both, None, None)
    return jax.shard_map(
        local,
        mesh=mesh,
        in_specs=(P(both, None),) + (rows3,) * 5 + (P(both, None), P()),
        out_specs=(rows3, rows3, P("blk", "head")),
        check_vma=False,
    )
```

time: 364 us -> 120 us (0.33)
  waiting for transfers between devices: 210 us -> 0 us
  Pallas kernels: 0 us -> 107 us
  matrix products: 44 us -> 0 us
  blocking collectives: 35.1 us -> 0 us
  starting transfers between devices: 31 us -> 0 us
  between operations: 14 us -> 0.73 us
  local copies, waits for them, and re-layouts: 19.2 us -> 6.4 us
  other arithmetic: 8.79 us -> 3.48 us
    reduce_scatter x1 -> x0, waiting for transfers between devices: 145 us -> none  [sum_by_axis(): so_far = lax.psum_scatter(so_far, axis, scatter_dimension=0, tiled=True)]
    pallas_call x0 -> x1, Pallas kernels: none -> 107 us  [local(): pl.pallas_call(kernel, out_shape=(jax.ShapeDtypeStruct((2, 20, TILE, 128)...]
    dot_general x26 -> x0, matrix products: 44 us -> none  [the longest x1 11 us: local(): lax.dot_general(gathered, value_rows, (((0,), (0,)), ((), ())), preferred...]
    all_to_all x1 -> x0, blocking collectives: 35.1 us -> none  [side_by_side(): lax.all_to_all(both, axis, split_axis=split_dim, concat_axis=concat_dim,...]
    all_to_all x3 -> x0, waiting for transfers between devices: 33.1 us -> none  [the longest x1 26.2 us: side_by_side(): lax.all_to_all(both, axis, split_axis=split_dim, concat_axis=concat_dim,...]
    ppermute x6 -> x0, waiting for transfers between devices: 30.8 us -> none  [the longest x2 27.7 us: shifted(): return lax.ppermute(x, axis, pairs)]
    ppermute x6 -> x0, starting transfers between devices: 20.4 us -> none  [the longest x2 10.7 us: with_halo(): lax.ppermute(lax.slice_in_dim(block, block.shape[dim] - width, None, axis...]
    all_to_all x3 -> x0, starting transfers between devices: 10.5 us -> none  [the longest x1 3.99 us: side_by_side(): lax.all_to_all(both, axis, split_axis=split_dim, concat_axis=concat_dim,...]
  transfers between devices with their start and end apart: 13 -> 0, of which waited for: 7 -> 0; matrix products, arithmetic and copies ran while one was open for 13% -> 0% of each run, Pallas kernels for 0% -> 0%
where the time goes in v2:
time: 120 us; the launch traced here: 118 us
  Pallas kernels  107 us (89%)
  local copies, waits for them, and re-layouts  6.4 us (5%)
  other arithmetic  3.48 us (3%)
    pallas_call x1, Pallas kernels, local(): pl.pallas_call(kernel, out_shape=(jax.ShapeDtypeStruct((2, 20, TILE, 128)...  107 us
    transpose x1, local copies, waits for them, and re-layouts, local(): return (jnp.swapaxes(grads[0], 0, 1), jnp.swapaxes(grads[1], 0, 1), weight)  2.53 us

profile of v2, /device:TPU:3, one launch (start us, length us, event | category | flops | bytes accessed | tf_op | source)
XLA Modules:
  0.0 117.8 jit_solution(3335366339756444955)
XLA Ops:
  0.6 0.0 copy-start.2
  0.6 0.0 copy-start
  0.7 0.9 pad_dynamic-slice_fusion
  1.5 0.1 compare_reduce_fusion
  1.7 0.1 copy.18
  1.7 1.7 %multiply_reduce_fusion = f32[128,20]{0,1:T(8,128)S(1)} fusion(bf16[128,20,128]{2,0,1:T(8,128)(2,1)} %param.13, bf16[128,20,128]{2,0,1:T(8,128)(2,1)} %param.12), kind=kLoop, calls=%fused_computation.2 | loop fusion | flops 1308160 | bytes 1320960 | tf_op jit(solution)/shard_map/reduce_sum | solution.py:421
  3.4 0.0 copy-done.2
  3.5 0.7 broadcast_in_dim.18.far
  4.2 0.6 pad.8.clone
  4.8 0.0 copy-done
  4.8 0.8 copy.19
  5.6 0.1 copy.23
  5.7 1.7 %pad_maximum_fusion.lt = bf16[4,2,16,80,128]{4,3,2,1,0:T(8,128)(2,1)} fusion(bf16[4,2,8,80,128]{4,3,2,1,0:T(8,128)(2,1)S(1)} %bitcast.26), kind=kLoop, calls=%fused_computation | loop fusion | flops 1310720 | bytes 3932160 | tf_op jit(solution)/shard_map/concatenate | solution.py:428
  7.4 107.2 %layer.1 = (bf16[2,20,128,128]{3,2,1,0:T(8,128)(2,1)}, f32[80,640]{1,0:T(8,128)}) custom-call(bf16[20,128,128]{2,1,0:T(8,128)(2,1)} %bitcast.28, bf16[20,128,128]{2,1,0:T(8,128)(2,1)} %bitcast.27, bf16[20,128,128]{2,1,0:T(8,128)(2,1)} %bitcast.29, bf16[20,128,128]{2,1,0:T(8,128)(2,1)} %bitcast.30, f32[4,5,8,128]{3,2,1,0:T(8,128)} %bitcast.31, ...), custom_call_target="tpu_custom_call" | custom-call | tf_op jit(solution)/shard_map/layer/pallas_call | solution.py:437
  114.5 0.0 copy-start.1
  114.6 2.5 %slice_bitcast_fusion = (bf16[128,20,128]{2,0,1:T(8,128)(2,1)}, bf16[128,20,128]{2,0,1:T(8,128)(2,1)}) fusion(bf16[2,20,128,128]{3,2,1,0:T(8,128)(2,1)} %get-tuple-element.5), kind=kLoop, calls=%fused_computation.3 | loop fusion | bytes 2621440 | tf_op jit(solution)/shard_map/transpose | solution.py:475
  117.1 0.0 copy-done.1
  117.1 0.7 copy.25
  (4 shorter events, 0.0 us)
Async XLA Ops:
  0.6 2.8 %copy-start.2 = (f32[128,20]{0,1:T(8,128)S(1)}, f32[128,20]{0,1:T(8,128)}, u32[]{:S(2)}) copy-start(f32[128,20]{0,1:T(8,128)} %param.14) | copy-start | bytes 30724
  0.6 4.2 %copy-start = (bf16[128,5120]{1,0:T(8,128)(2,1)S(1)}, bf16[128,5120]{1,0:T(8,128)(2,1)}, u32[]{:S(2)}) copy-start(bf16[128,5120]{1,0:T(8,128)(2,1)} %param.8) | copy-start | bytes 3932164
  114.5 2.5 %copy-start.1 = (f32[80,640]{1,0:T(8,128)S(1)}, f32[80,640]{1,0:T(8,128)}, u32[]{:S(2)}) copy-start(f32[80,640]{1,0:T(8,128)} %get-tuple-element.14) | copy-start | bytes 614404

commit v3 on v2

--- a/solution.py
+++ b/solution.py
@@ -50,7 +50,8 @@
 
 
 def kernel(
-    q_in, g_in, k_in, v_in, stat_in, far, lt, grads, weight,
+    q_in, g_in, k_in, v_in, lse_in, a_hbm, l_hbm, listed, query_out, key_out, weight,
+    a_in, l_in, lt, stat_in, far,
     win, kv, stat, entry_relay, gathered, dq, dk, dv, values, dq_out, dq_in, back, relay,
     x2_out, x2_in, xr_out, xr_in, xl_out, xl_in, total, z_out, z_in,
     y_send, y_recv, s_send, s_recv, h_send, h_recv, t_send, t_recv, l_send, l_recv,
@@ -72,12 +73,11 @@
         return pl.ds(pl.multiple_of(owner * 256, 256), 256)
 
     lane = pl.ds(pl.multiple_of(y * 256 + core * 128, 128), 128)
-    turn = pl.ds(lax.rem(z + 3, 8), 8)
-    own = []
-    for i, dx in enumerate(ORDER):
-        source = lt.at[lax.rem(x + dx, 4), core, turn]
-        own.append(pltpu.make_async_copy(source, gathered.at[i, :, :, lane], own_sem.at[i]))
-        own[-1].start()
+    grads = (query_out, key_out)
+    a_load = pltpu.make_async_copy(a_hbm, a_in, own_sem.at[0])
+    l_load = pltpu.make_async_copy(l_hbm, l_in, own_sem.at[1])
+    a_load.start()
+    l_load.start()
     meet(
         [{"blk": b, "head": yr}, {"blk": b, "head": yl}, {"blk": b, "head": y2}]
         + [{"blk": br, "head": y}, {"blk": bl, "head": y}]
@@ -116,14 +116,9 @@
             )
             sends[-1].start()
 
-    stat_sends = []
-    for i, where in enumerate((yr, yl, y2)):
-        stat_sends.append(
-            push(stat_in.at[where], stat.at[4 + y], s_send.at[i], s_recv.at[i], blk=b, head=where)
-        )
-        stat_sends[-1].start()
     keys = first(0, (k_in, v_in), kv, 0)
     halo = []
+    halo_stat = {}
 
     def pass_on(i, srcs, stat_src, owner):
         for j, (where, base, at) in enumerate(((br, 0, 0), (bl, 2 * SPAN, 8))):
@@ -135,44 +130,89 @@
                     )
                 )
                 halo[-1].start()
-            halo.append(
-                push(
-                    stat_src, stat.at[at + owner],
-                    t_send.at[i, j], t_recv.at[i, j], blk=where, head=y,
-                )
-            )
-            halo[-1].start()
+            if stat_src is not None:
+                stat_on(i, j, where, stat_src, at + owner)
+
+    def stat_on(i, j, where, stat_src, at):
+        halo_stat[i, j] = push(
+            stat_src, stat.at[at], t_send.at[i, j], t_recv.at[i, j], blk=where, head=y
+        )
+        halo_stat[i, j].start()
 
     def landed(owner):
         return [win.at[t, :, rows(SPAN + owner * TILE)] for t in range(2)]
 
-    pass_on(0, [mine(q_in, y), mine(g_in, y)], stat_in.at[y], y)
-    swaps = []
-    for i, dx in enumerate(ORDER):
-        swaps.append(
-            push(
-                lt.at[lax.rem(x + dx, 4), 1 - core, turn], gathered.at[i, :, :, lane],
-                l_send.at[i], l_recv.at[i], blk=mate, head=y,
-            )
-        )
-        swaps[-1].start()
+    pass_on(0, [mine(q_in, y), mine(g_in, y)], None, y)
     for h in range(HEADS):
         for t, (near, key) in enumerate(((q_in, k_in), (g_in, v_in))):
             win[t, h, rows(SPAN + y * TILE)] = near[y * HEADS + h]
             kv[t, h, rows(y * TILE)] = key[y * HEADS + h]
-    stat[4 + y] = stat_in[y]
+    a_load.wait()
+
+    def head_stat(h, carry):
+        product = g_in[h].astype(F32) * a_in[h].astype(F32)
+        delta = jnp.sum(product.T, axis=0, keepdims=True)
+        lse = lse_in[pl.ds(h, 1), :]
+        tile = jnp.concatenate([lse, delta, jnp.zeros((6, TILE), F32)], axis=0)
+        stat_in[h // HEADS, lax.rem(h, HEADS)] = tile
+        return carry
+
+    lax.fori_loop(0, 4 * HEADS, head_stat, 0)
     second(0, keys, kv, 0)
     queries = first(1, (q_in, g_in), win, SPAN)
+    stat[4 + y] = stat_in[y]
+    stat_sends = []
+    for i, where in enumerate((yr, yl, y2)):
+        stat_sends.append(
+            push(stat_in.at[where], stat.at[4 + y], s_send.at[i], s_recv.at[i], blk=b, head=where)
+        )
+        stat_sends[-1].start()
+    for j, (where, at) in enumerate(((br, 0), (bl, 8))):
+        stat_on(0, j, where, stat_in.at[y], at + y)
+
+    l_load.wait()
+    for j in range(40):
+        lt[128 * j : 128 * j + 128] = l_in[:, 128 * j : 128 * j + 128].T
+
+    def rows_of(dx, k, c):
+        to = (lax.rem(z + 3 + k, 8) * 4 + lax.rem(x + dx, 4)) * 2 + c
+        return pl.ds(pl.multiple_of(to * 80, 16), 80)
+
+    for i, dx in enumerate(ORDER):
+        for k in range(8):
+            gathered[i, k, :, lane] = lt[rows_of(dx, k, core)]
+    swaps = []
+    for i, dx in enumerate(ORDER):
+        for k in range(8):
+            swaps.append(
+                push(
+                    lt.at[rows_of(dx, k, 1 - core)], gathered.at[i, k, :, lane],
+                    l_send.at[i, k], l_recv.at[i, k], blk=mate, head=y,
+                )
+            )
+            swaps[-1].start()
+    for row in range(12):
+        block = b * 4 + (row - 4)
+        inside = (block >= 0) & (block < 4 * N_BLK)
+        at = jnp.clip(block, 0, 4 * N_BLK - 1)
+        entries = [listed[slot, at] for slot in range(8)]
+        lines = []
+        for k in range(4):
+            found = entries[0] == b * 4 + k
+            for entry in entries[1:]:
+                found = found | (entry == b * 4 + k)
+            gap = jnp.where(found & inside, jnp.float32(0.0), jnp.float32(FAR))
+            lines.append(jnp.full((1, TILE), gap, F32))
+        far[row] = jnp.concatenate(lines + lines, axis=0)
 
     pieces = ((0, 0), (0, 1), (1, 0), (2, 0), (3, 0), (1, 1), (2, 1), (3, 1))
     gathers = {}
-    for i in range(4):
-        own[i].wait()
 
     def spread(p):
         i, half = pieces[p]
         if p in (0, 2, 3, 4):
-            swaps[i].wait_recv()
+            for copy in swaps[8 * i : 8 * i + 8]:
+                copy.wait_recv()
         for j, where in enumerate((yr, yl)):
             piece = gathered.at[i, pl.ds(4 * half, 4), :, pair(y)]
             gathers[p, j] = push(
@@ -249,7 +289,7 @@
             dq_copies[-1].start()
 
     def halo_in(i):
-        for copy in halo[6 * i : 6 * i + 6]:
+        for copy in halo[4 * i : 4 * i + 4] + [halo_stat[i, 0], halo_stat[i, 1]]:
             copy.wait_recv()
 
     for copy in keys[2:]:
@@ -342,22 +382,22 @@
         back[0, h] = (
             dq[h] + dq_in[0, h].astype(F32) + dq_in[1, h].astype(F32)
         ).astype(BF16)
+    plan = [
+        (yr, back.at[0, :, rows(y2 * TILE)], relay.at[0]),
+        (yl, back.at[1, :, rows(y2 * TILE)], relay.at[1]),
+    ]
+    for t in range(2):
+        for where in (yr, yl):
+            plan.append((where, back.at[t, :, rows(where * TILE)], mine(grads[t], y)))
     back_copies = []
-    for i, (where, copy_from, copy_to) in enumerate(
-        (
-            (yr, back.at[0, :, rows(y2 * TILE)], relay.at[0]),
-            (yl, back.at[1, :, rows(y2 * TILE)], relay.at[1]),
-            (yr, back.at[:, :, rows(yr * TILE)], grads.at[:, pl.ds(y * HEADS, HEADS)]),
-            (yl, back.at[:, :, rows(yl * TILE)], grads.at[:, pl.ds(y * HEADS, HEADS)]),
-        )
-    ):
+    for i, (where, copy_from, copy_to) in enumerate(plan):
         back_copies.append(
             push(copy_from, copy_to, b_send.at[i], b_recv.at[i], blk=b, head=where)
         )
         back_copies[-1].start()
     for t in range(2):
         for h in range(HEADS):
-            grads[t, y * HEADS + h] = back[t, h, rows(y * TILE)]
+            grads[t][y * HEADS + h] = back[t, h, rows(y * TILE)]
 
     z_copies = {}
 
@@ -387,8 +427,8 @@
         back_copies[j].wait_recv()
         back_copies.append(
             push(
-                relay.at[j], grads.at[j, pl.ds(owner * HEADS, HEADS)],
-                b_send.at[4 + j], b_recv.at[4 + j], blk=b, head=where,
+                relay.at[j], mine(grads[j], owner),
+                b_send.at[6 + j], b_recv.at[6 + j], blk=b, head=where,
             )
         )
         back_copies[-1].start()
@@ -402,7 +442,7 @@
     for copy in back_copies[2:]:
         copy.wait_recv()
     copies = queries + keys + stat_sends + halo + swaps + list(gathers.values())
-    copies += list(x_copies.values()) + list(z_copies.values())
+    copies += list(x_copies.values()) + list(z_copies.values()) + list(halo_stat.values())
     for copy in copies + [value_copy] + dq_copies + back_copies:
         copy.wait_send()
 
@@ -418,31 +458,25 @@
 def local(
     layer_input, queries, key_vectors, value_vectors, out_grad, attn_out, log_sum, block_list
 ):
-    row_delta = jnp.sum(out_grad.astype(F32) * attn_out.astype(F32), axis=2)
-    stats = jnp.stack((log_sum.T, row_delta.T), axis=1)
-    stats = jnp.pad(stats, ((0, 0), (0, 6), (0, 0))).reshape(4, HEADS, 8, TILE)
     by_head = [
-        jnp.swapaxes(array, 0, 1) for array in (queries, out_grad, key_vectors, value_vectors)
+        jnp.swapaxes(array, 0, 1)
+        for array in (queries, out_grad, key_vectors, value_vectors, attn_out)
     ]
-    lt = jnp.transpose(layer_input.T.reshape(8, 4, 2, 80, TILE), (1, 2, 0, 3, 4))
-    lt = jnp.concatenate((lt, lt), axis=2)
-
-    first_block = lax.axis_index("blk") * 4
-    padded = jnp.pad(block_list, ((4, 4), (0, 0)), constant_values=-1)
-    lists = lax.dynamic_slice_in_dim(padded, first_block, 12, 0)
-    own_ids = first_block + jnp.arange(8, dtype=jnp.int32)
-    allowed = jnp.any(lists[:, None, :] == own_ids[None, :, None], axis=2)
-    far = jnp.broadcast_to(jnp.where(allowed, 0.0, FAR)[:, :, None], (12, 8, TILE)).astype(F32)
-
-    grads, weight = pl.pallas_call(
+    query_grad, key_grad, weight_grad = pl.pallas_call(
         kernel,
         out_shape=(
-            jax.ShapeDtypeStruct((2, 20, TILE, 128), BF16),
+            jax.ShapeDtypeStruct((20, TILE, 128), BF16),
+            jax.ShapeDtypeStruct((20, TILE, 128), BF16),
             jax.ShapeDtypeStruct((80, COLS), F32),
         ),
-        in_specs=[VMEM_SPEC] * 6 + [ANY_SPEC],
-        out_specs=[VMEM_SPEC] * 2,
+        in_specs=[VMEM_SPEC] * 5 + [ANY_SPEC] * 2 + [pl.BlockSpec(memory_space=pltpu.SMEM)],
+        out_specs=[VMEM_SPEC] * 3,
         scratch_shapes=[
+            pltpu.VMEM((20, TILE, 128), BF16),
+            pltpu.VMEM((TILE, 5120), BF16),
+            pltpu.VMEM((5120, TILE), BF16),
+            pltpu.VMEM((4, HEADS, 8, TILE), F32),
+            pltpu.VMEM((12, 8, TILE), F32),
             pltpu.VMEM((2, HEADS, 3 * SPAN, 128), BF16),
             pltpu.VMEM((2, HEADS, SPAN, 128), BF16),
             pltpu.VMEM((12, HEADS, 8, TILE), F32),
@@ -463,16 +497,16 @@
             pltpu.VMEM((8, 80, COLS), BF16),
             pltpu.VMEM((8, 80, COLS), BF16),
             sems(2, 8), sems(2, 8), sems(3), sems(3), sems(4, 2, 2), sems(4, 2, 2),
-            sems(4, 2), sems(4, 2), sems(4), sems(4),
-            sems(4), sems(8, 4), sems(8, 4), sems(), sems(), sems(4, 2), sems(4, 2),
-            sems(3, 4), sems(3, 4), sems(8), sems(8), sems(6), sems(6),
+            sems(4, 2), sems(4, 2), sems(4, 8), sems(4, 8),
+            sems(2), sems(8, 4), sems(8, 4), sems(), sems(), sems(4, 2), sems(4, 2),
+            sems(3, 4), sems(3, 4), sems(8), sems(8), sems(8), sems(8),
         ],
         compiler_params=pltpu.CompilerParams(
             collective_id=0, has_side_effects=True, vmem_limit_bytes=60 * 2**20
         ),
         name="layer",
-    )(*by_head, stats, far, lt)
-    return (jnp.swapaxes(grads[0], 0, 1), jnp.swapaxes(grads[1], 0, 1), weight)
+    )(*by_head[:4], log_sum.T, by_head[4], layer_input, block_list.T)
+    return (jnp.swapaxes(query_grad, 0, 1), jnp.swapaxes(key_grad, 0, 1), weight_grad)
 
 
 def solution(mesh):

time: 120 us -> 114 us (0.950)
  other arithmetic: 3.48 us -> 0 us
  local copies, waits for them, and re-layouts: 6.4 us -> 3.58 us
    transpose x1 -> x0, local copies, waits for them, and re-layouts: 2.53 us -> none  [local(): return (jnp.swapaxes(grads[0], 0, 1), jnp.swapaxes(grads[1], 0, 1), weight)]
    unnamed x9 -> x7, local copies, waits for them, and re-layouts: 1.48 us -> 3.58 us
    reduce_sum x1 -> x0, other arithmetic: 1.7 us -> none  [local(): row_delta = jnp.sum(out_grad.astype(F32) * attn_out.astype(F32), axis=2)]
    concatenate x1 -> x0, other arithmetic: 1.67 us -> none  [local(): lt = jnp.concatenate((lt, lt), axis=2)]
    pallas_call x1, Pallas kernels: 107 us -> 108 us  [local(): pl.pallas_call(kernel, out_shape=(jax.ShapeDtypeStruct((20, TILE, 128), B...]
where the time goes in v3:
time: 114 us; the launch traced here: 113 us
  Pallas kernels  108 us (95%)
  local copies, waits for them, and re-layouts  3.58 us (3%)
    pallas_call x1, Pallas kernels, local(): pl.pallas_call(kernel, out_shape=(jax.ShapeDtypeStruct((20, TILE, 128), B...  108 us
    unnamed x7, local copies, waits for them, and re-layouts  3.58 us

profile of v3, /device:TPU:3, one launch (start us, length us, event | category | flops | bytes accessed | tf_op | source)
XLA Modules:
  0.0 112.7 jit_solution(9645000536210705116)
XLA Ops:
  0.6 108.5 %layer.1 = (bf16[20,128,128]{2,1,0:T(8,128)(2,1)}, bf16[20,128,128]{2,1,0:T(8,128)(2,1)}, f32[80,640]{1,0:T(8,128)}) custom-call(bf16[20,128,128]{2,1,0:T(8,128)(2,1)} %bitcast.11, bf16[20,128,128]{2,1,0:T(8,128)(2,1)} %bitcast.12, bf16[20,128,128]{2,1,0:T(8,128)(2,1)} %bitcast.13, bf16[20,128,128]{2,1,0:T(8,128)(2,1)} %bitcast.14, f32[20,128]{1,0:T(8,128)} %bitcast.16, ...), custom_call_target="tpu_custom_call" | custom-call | tf_op jit(solution)/shard_map/layer/pallas_call | solution.py:465
  109.1 0.0 copy-start
  109.1 0.0 copy-start.1
  109.1 2.1 %copy.14 = bf16[128,20,128]{2,0,1:T(8,128)(2,1)} copy(bf16[128,20,128]{2,0,1:T(8,128)(2,1)} %bitcast.10) | data formatting | bytes 1310720
  111.2 0.0 copy-done
  111.2 0.8 copy.15
  112.0 0.0 copy-done.1
  112.0 0.7 copy.16
Async XLA Ops:
  109.1 2.1 %copy-start = (bf16[20,128,128]{2,1,0:T(8,128)(2,1)S(1)}, bf16[20,128,128]{2,1,0:T(8,128)(2,1)}, u32[]{:S(2)}) copy-start(bf16[20,128,128]{2,1,0:T(8,128)(2,1)} %get-tuple-element.7) | copy-start | bytes 1966084
  109.1 2.9 %copy-start.1 = (f32[80,640]{1,0:T(8,128)S(1)}, f32[80,640]{1,0:T(8,128)}, u32[]{:S(2)}) copy-start(f32[80,640]{1,0:T(8,128)} %get-tuple-element.14) | copy-start | bytes 614404

commit v4 on v3

--- a/solution.py
+++ b/solution.py
@@ -305,18 +305,19 @@
         queries[4 + i].wait_recv()
         stat_sends[i].wait_recv()
         pass_on(1 + i, landed(owner), stat.at[4 + owner], owner)
-    send_dq(0, y)
-    halo_in(1)
-    attend(yl, False)
     queries[6].wait_recv()
     queries[7].wait_recv()
     stat_sends[2].wait_recv()
     pass_on(3, landed(y2), stat.at[4 + y2], y2)
+    send_dq(0, y)
+    halo_in(1)
+    attend(yl, False)
     send_dq(1, yl)
+    forward(0)
     halo_in(2)
     attend(yr, False)
     send_dq(2, yr)
-    forward(0)
+    forward(1)
     spread(3)
     halo_in(3)
     attend(y2, False)
@@ -329,12 +330,8 @@
         values.at[:, core], values.at[:, core], v_send, v_recv, blk=mate, head=y
     )
     value_copy.start()
-    send_dq(3, y2)
-    forward(1)
     forward(2)
     spread(4)
-    forward(3)
-    spread(5)
     value_copy.wait_recv()
     x_copies = {}
 
@@ -352,6 +349,9 @@
     for q, part in quarters(product(1)):
         x2_out[2 + q] = part.astype(BF16)
         x_push("far", 0, 2 + q, x2_out, x2_in, xl)
+    send_dq(3, y2)
+    forward(3)
+    spread(5)
     for h in range(HEADS):
         back[1, h] = (dk[h] * SCALE).astype(BF16)
     forward(4)

time: 114 us -> 111 us (0.974)
  Pallas kernels: 108 us -> 106 us
    pallas_call x1, Pallas kernels: 108 us -> 106 us  [local(): pl.pallas_call(kernel, out_shape=(jax.ShapeDtypeStruct((20, TILE, 128), B...]
where the time goes in v4:
time: 111 us; the launch traced here: 110 us
  Pallas kernels  106 us (95%)
  local copies, waits for them, and re-layouts  3.58 us (3%)
    pallas_call x1, Pallas kernels, local(): pl.pallas_call(kernel, out_shape=(jax.ShapeDtypeStruct((20, TILE, 128), B...  106 us
    unnamed x7, local copies, waits for them, and re-layouts  3.58 us

profile of v4, /device:TPU:3, one launch (start us, length us, event | category | flops | bytes accessed | tf_op | source)
XLA Modules:
  0.0 110.2 jit_solution(16669661506407428075)
XLA Ops:
  0.6 105.9 %layer.1 = (bf16[20,128,128]{2,1,0:T(8,128)(2,1)}, bf16[20,128,128]{2,1,0:T(8,128)(2,1)}, f32[80,640]{1,0:T(8,128)}) custom-call(bf16[20,128,128]{2,1,0:T(8,128)(2,1)} %bitcast.11, bf16[20,128,128]{2,1,0:T(8,128)(2,1)} %bitcast.12, bf16[20,128,128]{2,1,0:T(8,128)(2,1)} %bitcast.13, bf16[20,128,128]{2,1,0:T(8,128)(2,1)} %bitcast.14, f32[20,128]{1,0:T(8,128)} %bitcast.16, ...), custom_call_target="tpu_custom_call" | custom-call | tf_op jit(solution)/shard_map/layer/pallas_call | solution.py:465
  106.6 0.0 copy-start
  106.6 0.0 copy-start.1
  106.6 2.1 %copy.14 = bf16[128,20,128]{2,0,1:T(8,128)(2,1)} copy(bf16[128,20,128]{2,0,1:T(8,128)(2,1)} %bitcast.10) | data formatting | bytes 1310720
  108.7 0.0 copy-done
  108.7 0.8 copy.15
  109.5 0.0 copy-done.1
  109.5 0.7 copy.16
Async XLA Ops:
  106.6 2.1 %copy-start = (bf16[20,128,128]{2,1,0:T(8,128)(2,1)S(1)}, bf16[20,128,128]{2,1,0:T(8,128)(2,1)}, u32[]{:S(2)}) copy-start(bf16[20,128,128]{2,1,0:T(8,128)(2,1)} %get-tuple-element.7) | copy-start | bytes 1966084
  106.6 2.9 %copy-start.1 = (f32[80,640]{1,0:T(8,128)S(1)}, f32[80,640]{1,0:T(8,128)}, u32[]{:S(2)}) copy-start(f32[80,640]{1,0:T(8,128)} %get-tuple-element.14) | copy-start | bytes 614404

commit v5 on v4

--- a/solution.py
+++ b/solution.py
@@ -50,8 +50,8 @@
 
 
 def kernel(
-    q_in, g_in, k_in, v_in, lse_in, a_hbm, l_hbm, listed, query_out, key_out, weight,
-    a_in, l_in, lt, stat_in, far,
+    q_hbm, g_hbm, k_in, v_in, lse_in, a_hbm, l_hbm, listed, query_out, key_out, weight,
+    q_in, g_in, a_in, l_in, lt, stat_in, far,
     win, kv, stat, entry_relay, gathered, dq, dk, dv, values, dq_out, dq_in, back, relay,
     x2_out, x2_in, xr_out, xr_in, xl_out, xl_in, total, z_out, z_in,
     y_send, y_recv, s_send, s_recv, h_send, h_recv, t_send, t_recv, l_send, l_recv,
@@ -74,6 +74,10 @@
 
     lane = pl.ds(pl.multiple_of(y * 256 + core * 128, 128), 128)
     grads = (query_out, key_out)
+    q_load = pltpu.make_async_copy(q_hbm, q_in, own_sem.at[2])
+    g_load = pltpu.make_async_copy(g_hbm, g_in, own_sem.at[3])
+    q_load.start()
+    g_load.start()
     a_load = pltpu.make_async_copy(a_hbm, a_in, own_sem.at[0])
     l_load = pltpu.make_async_copy(l_hbm, l_in, own_sem.at[1])
     a_load.start()
@@ -142,6 +146,8 @@
     def landed(owner):
         return [win.at[t, :, rows(SPAN + owner * TILE)] for t in range(2)]
 
+    q_load.wait()
+    g_load.wait()
     pass_on(0, [mine(q_in, y), mine(g_in, y)], None, y)
     for h in range(HEADS):
         for t, (near, key) in enumerate(((q_in, k_in), (g_in, v_in))):
@@ -237,17 +243,17 @@
         left = gathered[i, 4 * half : 4 * half + 4].reshape(HALF, 1024)
         return dot(left, values[...].reshape(1024, COLS), ((1,), (0,)))
 
-    def attend(owner, lead):
-        spans = [rows(part * SPAN + owner * TILE) for part in range(3)]
+    def attend(tiles_of, lead):
+        spans = [rows(part * SPAN + owner * TILE) for part, owner in tiles_of]
 
         def one_head(h, carry):
             key, val = kv[0, h], kv[1, h]
             query = jnp.concatenate([win[0, h, at] for at in spans], axis=0)
             grad = jnp.concatenate([win[1, h, at] for at in spans], axis=0)
-            tiles = [stat[4 * part + owner, h] for part in range(3)]
+            tiles = [stat[4 * part + owner, h] for part, owner in tiles_of]
             lse = jnp.concatenate([tile[0:1] for tile in tiles], axis=1)
             delta = jnp.concatenate([tile[1:2] for tile in tiles], axis=1)
-            apart = jnp.concatenate([far[4 * part + owner, 0:4] for part in range(3)], axis=1) + lse
+            apart = jnp.concatenate([far[4 * part + owner, 0:4] for part, owner in tiles_of], axis=1) + lse
             scores = dot(key, query, ((1,), (1,))) * SCALE
             dweights = dot(val, grad, ((1,), (1,)))
             weights = jnp.concatenate(
@@ -262,9 +268,12 @@
             value_part = dot(weights, grad, ((1,), (0,)))
             key_part = dot(dscores, query, ((1,), (0,)))
             query_part = dot(dscores, key, ((0,), (0,))) * SCALE
-            dq_out[0, h, rows(owner * TILE)] = query_part[:TILE].astype(BF16)
-            dq[h, rows(owner * TILE)] = query_part[TILE : 2 * TILE]
-            dq_out[1, h, rows(owner * TILE)] = query_part[2 * TILE :].astype(BF16)
+            for n, (part, owner) in enumerate(tiles_of):
+                piece = query_part[n * TILE : (n + 1) * TILE]
+                if part == 1:
+                    dq[h, rows(owner * TILE)] = piece
+                else:
+                    dq_out[part // 2, h, rows(owner * TILE)] = piece.astype(BF16)
             if lead:
                 dv[h] = value_part
                 dk[h] = key_part
@@ -299,28 +308,29 @@
     spread(1)
     spread(2)
     halo_in(0)
-    attend(y, True)
+    attend([(0, y), (1, y), (2, y)], True)
     for i, owner in ((0, yl), (1, yr)):
         queries[2 + i].wait_recv()
         queries[4 + i].wait_recv()
         stat_sends[i].wait_recv()
         pass_on(1 + i, landed(owner), stat.at[4 + owner], owner)
+    attend([(1, yl), (1, yr)], False)
     queries[6].wait_recv()
     queries[7].wait_recv()
     stat_sends[2].wait_recv()
     pass_on(3, landed(y2), stat.at[4 + y2], y2)
     send_dq(0, y)
     halo_in(1)
-    attend(yl, False)
+    attend([(0, yl), (2, yl), (1, y2)], False)
     send_dq(1, yl)
     forward(0)
     halo_in(2)
-    attend(yr, False)
+    attend([(0, yr), (2, yr)], False)
     send_dq(2, yr)
     forward(1)
     spread(3)
     halo_in(3)
-    attend(y2, False)
+    attend([(0, y2), (2, y2)], False)
 
     for h in range(HEADS):
         cols = pl.ds(h * 128, 128)
@@ -333,6 +343,20 @@
     forward(2)
     spread(4)
     value_copy.wait_recv()
+    plan = [
+        (yr, back.at[0, :, rows(y2 * TILE)], relay.at[0]),
+        (yl, back.at[1, :, rows(y2 * TILE)], relay.at[1]),
+    ]
+    for t in range(2):
+        for where in (yr, yl):
+            plan.append((where, back.at[t, :, rows(where * TILE)], mine(grads[t], y)))
+    back_copies = {}
+
+    def send_back(i):
+        where, copy_from, copy_to = plan[i]
+        back_copies[i] = push(copy_from, copy_to, b_send.at[i], b_recv.at[i], blk=b, head=where)
+        back_copies[i].start()
+
     x_copies = {}
 
     def x_push(name, i, q, src, dst, where):
@@ -374,6 +398,8 @@
         x_copies["far", 2 + q].wait_recv()
         xl_out[2 + q] = (part + x2_in[2 + q].astype(F32)).astype(BF16)
         x_push("left", 2, 2 + q, xl_out, xl_in, xl)
+    for i in (1, 4, 5):
+        send_back(i)
     forward(7)
 
     for copy in dq_copies:
@@ -382,19 +408,8 @@
         back[0, h] = (
             dq[h] + dq_in[0, h].astype(F32) + dq_in[1, h].astype(F32)
         ).astype(BF16)
-    plan = [
-        (yr, back.at[0, :, rows(y2 * TILE)], relay.at[0]),
-        (yl, back.at[1, :, rows(y2 * TILE)], relay.at[1]),
-    ]
-    for t in range(2):
-        for where in (yr, yl):
-            plan.append((where, back.at[t, :, rows(where * TILE)], mine(grads[t], y)))
-    back_copies = []
-    for i, (where, copy_from, copy_to) in enumerate(plan):
-        back_copies.append(
-            push(copy_from, copy_to, b_send.at[i], b_recv.at[i], blk=b, head=where)
-        )
-        back_copies[-1].start()
+    for i in (0, 2, 3):
+        send_back(i)
     for t in range(2):
         for h in range(HEADS):
             grads[t][y * HEADS + h] = back[t, h, rows(y * TILE)]
@@ -425,25 +440,22 @@
     reduce_quarter(2)
     for j, (where, owner) in enumerate(((yr, yl), (yl, yr))):
         back_copies[j].wait_recv()
-        back_copies.append(
-            push(
-                relay.at[j], mine(grads[j], owner),
-                b_send.at[6 + j], b_recv.at[6 + j], blk=b, head=where,
-            )
+        back_copies[6 + j] = push(
+            relay.at[j], mine(grads[j], owner),
+            b_send.at[6 + j], b_recv.at[6 + j], blk=b, head=where,
         )
-        back_copies[-1].start()
-
+        back_copies[6 + j].start()
     reduce_quarter(3)
     result = weight[...]
     for r in (3, 4, 5, 6, 7, 1, 2):
         z_copies[r].wait_recv()
         result = result + z_in[r].astype(F32)
     weight[...] = result
-    for copy in back_copies[2:]:
-        copy.wait_recv()
+    for i in range(2, 8):
+        back_copies[i].wait_recv()
     copies = queries + keys + stat_sends + halo + swaps + list(gathers.values())
     copies += list(x_copies.values()) + list(z_copies.values()) + list(halo_stat.values())
-    for copy in copies + [value_copy] + dq_copies + back_copies:
+    for copy in copies + [value_copy] + dq_copies + list(back_copies.values()):
         copy.wait_send()
 
 
@@ -469,9 +481,11 @@
             jax.ShapeDtypeStruct((20, TILE, 128), BF16),
             jax.ShapeDtypeStruct((80, COLS), F32),
         ),
-        in_specs=[VMEM_SPEC] * 5 + [ANY_SPEC] * 2 + [pl.BlockSpec(memory_space=pltpu.SMEM)],
+        in_specs=[ANY_SPEC] * 2 + [VMEM_SPEC] * 3 + [ANY_SPEC] * 2 + [pl.BlockSpec(memory_space=pltpu.SMEM)],
         out_specs=[VMEM_SPEC] * 3,
         scratch_shapes=[
+            pltpu.VMEM((20, TILE, 128), BF16),
+            pltpu.VMEM((20, TILE, 128), BF16),
             pltpu.VMEM((20, TILE, 128), BF16),
             pltpu.VMEM((TILE, 5120), BF16),
             pltpu.VMEM((5120, TILE), BF16),
@@ -498,7 +512,7 @@
             pltpu.VMEM((8, 80, COLS), BF16),
             sems(2, 8), sems(2, 8), sems(3), sems(3), sems(4, 2, 2), sems(4, 2, 2),
             sems(4, 2), sems(4, 2), sems(4, 8), sems(4, 8),
-            sems(2), sems(8, 4), sems(8, 4), sems(), sems(), sems(4, 2), sems(4, 2),
+            sems(4), sems(8, 4), sems(8, 4), sems(), sems(), sems(4, 2), sems(4, 2),
             sems(3, 4), sems(3, 4), sems(8), sems(8), sems(8), sems(8),
         ],
         compiler_params=pltpu.CompilerParams(

time: 111 us -> 111 us (level)
  no operation moved by 1% of the time
where the time goes in v5:
time: 111 us; the launch traced here: 110 us
  Pallas kernels  106 us (95%)
  local copies, waits for them, and re-layouts  3.58 us (3%)
    pallas_call x1, Pallas kernels, local(): pl.pallas_call(kernel, out_shape=(jax.ShapeDtypeStruct((20, TILE, 128), B...  106 us
    unnamed x7, local copies, waits for them, and re-layouts  3.58 us

profile of v5, /device:TPU:3, one launch (start us, length us, event | category | flops | bytes accessed | tf_op | source)
XLA Modules:
  0.0 110.3 jit_solution(3784268227509650813)
XLA Ops:
  0.6 106.0 %layer.1 = (bf16[20,128,128]{2,1,0:T(8,128)(2,1)}, bf16[20,128,128]{2,1,0:T(8,128)(2,1)}, f32[80,640]{1,0:T(8,128)}) custom-call(bf16[20,128,128]{2,1,0:T(8,128)(2,1)} %bitcast.11, bf16[20,128,128]{2,1,0:T(8,128)(2,1)} %bitcast.12, bf16[20,128,128]{2,1,0:T(8,128)(2,1)} %bitcast.13, bf16[20,128,128]{2,1,0:T(8,128)(2,1)} %bitcast.14, f32[20,128]{1,0:T(8,128)} %bitcast.16, ...), custom_call_target="tpu_custom_call" | custom-call | tf_op jit(solution)/shard_map/layer/pallas_call | solution.py:477
  106.7 0.0 copy-start
  106.7 0.0 copy-start.1
  106.7 2.1 %copy.14 = bf16[128,20,128]{2,0,1:T(8,128)(2,1)} copy(bf16[128,20,128]{2,0,1:T(8,128)(2,1)} %bitcast.10) | data formatting | bytes 1310720
  108.7 0.0 copy-done
  108.7 0.8 copy.15
  109.6 0.0 copy-done.1
  109.6 0.7 copy.16
Async XLA Ops:
  106.7 2.1 %copy-start = (bf16[20,128,128]{2,1,0:T(8,128)(2,1)S(1)}, bf16[20,128,128]{2,1,0:T(8,128)(2,1)}, u32[]{:S(2)}) copy-start(bf16[20,128,128]{2,1,0:T(8,128)(2,1)} %get-tuple-element.7) | copy-start | bytes 1966084
  106.7 2.9 %copy-start.1 = (f32[80,640]{1,0:T(8,128)S(1)}, f32[80,640]{1,0:T(8,128)}, u32[]{:S(2)}) copy-start(f32[80,640]{1,0:T(8,128)} %get-tuple-element.14) | copy-start | bytes 614404
